TPU v7x, 128 devices: a whole 4x4x4 slice. The times are simulated.
128 devices in a mesh: fsdp: 8 (over z_hi, y), tp: 16 (over z_lo, x, core).
Axes of the slice: x: 4, y: 4, z: 4 (z_hi: 2, z_lo: 2; z = z_hi * 2 + z_lo), core: 2. Of those that a mesh axis runs over, the one named last changes fastest.
Arguments:
- tokens: bfloat16 [2048, 8192], P('fsdp', 'tp'), may hold values from -6 to 6
- out_grad: bfloat16 [2048, 8192], P('fsdp', 'tp'), may hold values from -6 to 6
- gate_weight: bfloat16 [8192, 2048], P('fsdp', 'tp'), may hold values from -0.0625 to 0.0625
- up_weight: bfloat16 [8192, 2048], P('fsdp', 'tp'), may hold values from -0.0625 to 0.0625
- down_weight: bfloat16 [2048, 8192], P('tp', 'fsdp'), may hold values from -0.125 to 0.125
Outputs:
- input_grad: bfloat16 [2048, 8192], P('fsdp', 'tp')
- gate_grad: float32 [8192, 2048], P('fsdp', 'tp')
- up_grad: float32 [8192, 2048], P('fsdp', 'tp')
- down_grad: float32 [2048, 8192], P('tp', 'fsdp')
All inputs are finite; a program needn't handle non-finite values.
Results may differ from a plain program's by a relative error of at most 0.0023.
Values may be sent and summed in bfloat16 or wider, within the bound.
A program may use at most 128 MiB of HBM per device.

v0:
```python
import math

import jax
import jax.numpy as jnp
from jax import lax
from jax.sharding import Mesh
from jax.sharding import PartitionSpec as P

FSDP = ("fsdp_0", "fsdp_1")


def laid_out(parts, dim):
    parts = jnp.moveaxis(parts, 0, dim)
    dims = parts.shape
    return parts.reshape(*dims[:dim], dims[dim] * dims[dim + 1], *dims[dim + 2 :])


def one_gather(arrays, axis, dims):
    line = jnp.concatenate([a.reshape(-1) for a in arrays])
    lines, at, outs = lax.all_gather(line, axis), 0, []
    for a, dim in zip(arrays, dims):
        parts = lines[:, at : at + a.size].reshape(-1, *a.shape)
        outs.append(laid_out(parts, dim))
        at += a.size
    return tuple(outs)


def stacked_from(value, axes, turns):
    parts = value[None]
    for k in turns:
        parts = lax.all_gather(parts, axes[k], axis=0, tiled=True)
    current = [lax.axis_size(axes[k]) for k in reversed(turns)]
    parts = parts.reshape(*current, *value.shape)
    turned = sorted(range(len(turns)), key=lambda place: turns[len(turns) - 1 - place])
    return parts.transpose(*turned, *range(len(turns), parts.ndim)).reshape(-1, *value.shape)


def gathered_by_axis(value, axes, turns, dim):
    return laid_out(stacked_from(value, axes, turns), dim)


def taken_in(value, axes, turns, dim, absorb, carry):
    everything = jax.tree.map(lambda part: gathered_by_axis(part, axes, turns, dim), value)
    return absorb(carry, everything, jnp.int32(0))


def own_rows(portion, rows, axis):
    count = rows * lax.axis_size(axis)
    return lax.psum_scatter(portion(jnp.int32(0), count), axis, scatter_dimension=0, tiled=True)


def column_term(left, right, start, count, factor):
    block = lax.dynamic_slice_in_dim(left, start, count, 1)
    product = lax.dot_general(
        block, right, (((0,), (0,)), ((), ())), preferred_element_type=jnp.float32
    )
    return product * factor


def shards(tokens, out_grad, gate_weight, up_weight, down_weight):
    factor = 1.0 / math.sqrt(tokens.shape[0] * lax.axis_size(FSDP))
    whole = lax.all_gather(tokens, "tp", axis=1, tiled=True)
    grads = lax.all_gather(out_grad, "tp", axis=1, tiled=True)
    gate_full, up_full = one_gather((gate_weight, up_weight), FSDP, (0, 0))
    gate = jnp.dot(whole, gate_full, preferred_element_type=jnp.float32)
    up = jnp.dot(whole, up_full, preferred_element_type=jnp.float32)

    def add_down(total, piece, start):
        columns = lax.dynamic_slice_in_dim(grads, start, piece.shape[1], 1)
        return total + lax.dot_general(
            columns, piece, (((1,), (1,)), ((), ())), preferred_element_type=jnp.float32
        )

    initial = jnp.zeros((whole.shape[0], down_weight.shape[0]), jnp.float32)
    hidden_grad = taken_in(down_weight, FSDP, (0, 1), 1, add_down, initial)
    squashed = jax.nn.sigmoid(gate)
    activated = gate * squashed
    slope = squashed * (1.0 + gate * (1.0 - squashed))
    hidden = (activated * up).astype(jnp.bfloat16)
    gate_delta = (hidden_grad * up * slope).astype(jnp.bfloat16)
    up_delta = (hidden_grad * activated).astype(jnp.bfloat16)

    def rows_term(start, count):
        gate_rows = lax.dynamic_slice_in_dim(gate_full, start, count, 0)
        up_rows = lax.dynamic_slice_in_dim(up_full, start, count, 0)
        first = lax.dot_general(
            gate_rows, gate_delta, (((1,), (1,)), ((), ())), preferred_element_type=jnp.float32
        )
        second = lax.dot_general(
            up_rows, up_delta, (((1,), (1,)), ((), ())), preferred_element_type=jnp.float32
        )
        return first + second

    local_rows = own_rows(rows_term, tokens.shape[1], "tp")
    input_grad = local_rows.T.astype(jnp.bfloat16)
    rows_here = gate_weight.shape[0]

    def joint_term(start, count):
        return jnp.concatenate(
            [
                column_term(whole, gate_delta, start, count, factor),
                column_term(whole, up_delta, start, count, factor),
                column_term(grads, hidden, start, count, factor),
            ],
            axis=1,
        )

    summed = own_rows(joint_term, rows_here, FSDP)
    width = gate_delta.shape[1]
    gate_grad = summed[:, :width]
    up_grad = summed[:, width : 2 * width]
    down_grad = summed[:, 2 * width :].T
    return (input_grad, gate_grad, up_grad, down_grad)


def solution(mesh):
    finer = Mesh(mesh.devices.reshape(2, 4, mesh.shape["tp"]), ("fsdp_0", "fsdp_1", "tp"))
    return jax.shard_map(
        shards,
        mesh=finer,
        in_specs=(P(FSDP, "tp"), P(FSDP, "tp"), P(FSDP, "tp"), P(FSDP, "tp"), P("tp", FSDP)),
        out_specs=(P(FSDP, "tp"), P(FSDP, "tp"), P(FSDP, "tp"), P("tp", FSDP)),
        check_vma=False,
    )
```

profile of v0, /device:TPU:1, one launch (start us, length us, event | category | flops | bytes accessed | tf_op | source)
XLA Modules:
  0.0 449.4 jit_solution(1478735136044264735)
XLA Ops:
  7.2 13.1 %all-gather.1 = bf16[256,1024]{1,0:T(8,128)(2,1)} all-gather(bf16[128,1024]{1,0:T(8,128)(2,1)} %param.9), channel_id=3, replica_groups=mesh['fsdp_0'=2,'fsdp_1'=4,'tp'=16] {'fsdp_0'}, dimensions={0}, use_global_device_ids=true | all-gather | bytes 786432 | tf_op jit(solution)/shard_map/all_gather | solution.py:31
  20.4 1.9 pad_maximum_fusion.1
  22.3 0.7 all-gather.11.cloned.1.call-update
  23.0 0.5 all-gather.7.cloned.1.call-update
  23.6 28.2 %all-gather.9.cloned.1.call-done = bf16[8,128,1024]{2,1,0:T(8,128)(2,1)} async-done(((bf16[2,128,1024]{2,1,0:T(8,128)(2,1)}), bf16[8,128,1024]{2,1,0:T(8,128)(2,1)}) %all-gather.9.cloned.1.call-update) | async-done | bytes 2097168 | tf_op jit(solution)/shard_map/all_gather | solution.py:31
  51.8 1.9 copy.27
  53.7 2.4 copy.28
  56.1 69.4 %all-gather.13.cloned.1.call-done = bf16[2097152]{0:T(1024)(128)(2,1)} async-done(((bf16[262144]{0:T(1024)(128)(2,1)}), bf16[2097152]{0:T(1024)(128)(2,1)}) %all-gather.13.cloned.1.call-update) | async-done | bytes 4194320 | tf_op jit(solution)/shard_map/all_gather | solution.py:20
  125.4 5.9 %reshape.28 = bf16[8,262144]{1,0:T(8,128)(2,1)} reshape(bf16[2097152]{0:T(1024)(128)(2,1)} %all-gather.13.cloned.1.call-done) | data formatting | bytes 8388608 | tf_op jit(solution)/shard_map/all_gather | solution.py:20
  131.3 3.9 fusion.6
  135.2 2.3 reshape_reshape.6
  137.5 2.5 reshape_reshape.7
  140.0 23.3 %all-gather.11.cloned.1.call-done = bf16[256,8192]{1,0:T(8,128)(2,1)} async-done(((bf16[256,512]{1,0:T(8,128)(2,1)}), bf16[256,8192]{1,0:T(8,128)(2,1)}) %all-gather.11.cloned.1.call-update) | async-done | bytes 4194320 | tf_op jit(solution)/shard_map/all_gather | solution.py:62
  163.4 4.2 convolution_bitcast_fusion
  167.6 1.3 convolution_bitcast_fusion.1
  169.0 33.2 %all-gather.7.cloned.1.call-done = bf16[256,8192]{1,0:T(8,128)(2,1)} async-done(((bf16[256,512]{1,0:T(8,128)(2,1)}), bf16[256,8192]{1,0:T(8,128)(2,1)}) %all-gather.7.cloned.1.call-update) | async-done | bytes 4194320 | tf_op jit(solution)/shard_map/all_gather | solution.py:63
  202.2 4.2 multiply_convert_fusion.1
  206.4 1.2 fusion.7
  207.7 4.5 %convolution_add_fusion = f32[8192,256]{1,0:T(8,128)} fusion(f32[8192,256]{1,0:T(8,128)S(1)} %fusion.7, bf16[8192,128]{1,0:T(8,128)(2,1)S(1)} %reshape_reshape.7, bf16[256,128]{1,0:T(8,128)(2,1)S(1)} %get-tuple-element.25), kind=kOutput, calls=%fused_computation.1 | convolution fusion | flops 538968064 | bytes 18939904 | tf_op jit(solution)/shard_map/dot_general | solution.py:89
  212.2 0.2 reduce-scatter.5.cloned.1.call-start
  212.4 3.3 fusion.1
  215.9 0.9 fusion.2
  216.8 1.3 copy-done.3
  218.1 1.0 fusion
  219.0 5.0 %pad_maximum_fusion = f32[8192,384]{0,1:T(8,128)} fusion(f32[8192,128]{0,1:T(8,128)S(1)} %fusion, f32[8192,128]{0,1:T(8,128)S(1)} %fusion.1, f32[8192,128]{0,1:T(8,128)S(1)} %fusion.2), kind=kLoop, calls=%fused_computation | loop fusion | flops 6291456 | bytes 25165824 | tf_op jit(solution)/shard_map/concatenate | solution.py:99
  224.0 59.2 %reduce-scatter.3.cloned.1.call-done = f32[512,256]{1,0:T(8,128)} async-done(((f32[8192,256]{1,0:T(8,128)}), f32[512,256]{1,0:T(8,128)}) %reduce-scatter.3.cloned.1.call-update) | async-done | bytes 524304 | tf_op jit(solution)/shard_map/reduce_scatter | solution.py:49
  283.2 1.1 convert_bitcast_fusion
  284.3 0.8 copy.31
  285.1 153.2 %reduce-scatter.5.cloned.1.call-done = f32[1024,384]{0,1:T(8,128)} async-done(((f32[8192,384]{0,1:T(8,128)}), f32[1024,384]{0,1:T(8,128)}) %reduce-scatter.5.cloned.1.call-update) | async-done | bytes 1572880 | tf_op jit(solution)/shard_map/reduce_scatter | solution.py:49
  438.3 2.3 slice_bitcast_fusion
  440.6 1.0 copy.32
  441.6 1.0 copy.33
  (16 shorter events, 0.5 us)
Async XLA Ops:
  7.2 44.6 %all-gather.9.cloned.1.call-start = ((), (), s32[]{:S(2)}) async-start(), calls=%async_computation.3 | async-start | bytes 2621440 | tf_op jit(solution)/shard_map/all_gather | solution.py:31
  20.3 105.1 %all-gather.13.cloned.1.call-start = ((), (), s32[]{:S(2)}) async-start(), calls=%async_computation.7 | async-start | bytes 4718592 | tf_op jit(solution)/shard_map/all_gather | solution.py:20
  22.2 141.1 %all-gather.11.cloned.1.call-start = ((), (), s32[]{:S(2)}) async-start(), calls=%async_computation.4 | async-start | bytes 4456448 | tf_op jit(solution)/shard_map/all_gather | solution.py:62
  23.0 179.2 %all-gather.7.cloned.1.call-start = ((), (), s32[]{:S(2)}) async-start(), calls=%async_computation.2 | async-start | bytes 4456448 | tf_op jit(solution)/shard_map/all_gather | solution.py:63
  23.6 259.7 %reduce-scatter.3.cloned.1.call-start = ((), (), s32[]{:S(2)}) async-start(), calls=%async_computation.5 | async-start | bytes 8912896 | tf_op jit(solution)/shard_map/reduce_scatter | solution.py:49
  163.4 4.3 copy-start
  202.1 4.3 copy-start.2
  212.2 226.1 %reduce-scatter.5.cloned.1.call-start = ((), (), s32[]{:S(2)}) async-start(), calls=%async_computation.6 | async-start | bytes 14155776 | tf_op jit(solution)/shard_map/reduce_scatter | solution.py:49
  212.4 3.5 copy-start.1
  215.9 2.2 copy-start.3
Sparse Core Ops, SparseCore 0:
  20.4 31.3 all-gather.8
  54.7 70.7 all-gather.12
  127.1 36.1 all-gather.10
  164.9 37.2 all-gather.6
  212.3 70.8 reduce-scatter.2
  287.0 151.2 reduce-scatter.4
where the time goes:
time: 450 us; the launch traced here: 449 us
  waiting for transfers between devices  368 us (82%)
  local copies, waits for them, and re-layouts  25.4 us (6%)
  matrix products  20.7 us (5%)
  between operations  14.2 us (3%)
  blocking collectives  13.1 us (3%)
  other arithmetic  7.91 us (2%)
    reduce_scatter x2, waiting for transfers between devices, own_rows(): lax.psum_scatter(portion(jnp.int32(0), count), axis, scatter_dimension=0,...  212 us
    all_gather x1, waiting for transfers between devices, one_gather(): lines, at, outs = (lax.all_gather(line, axis), 0, [])  69.4 us
    all_gather x1, waiting for transfers between devices, shards(): grads = lax.all_gather(out_grad, 'tp', axis=1, tiled=True)  33.2 us
    all_gather x1, waiting for transfers between devices, stacked_from(): parts = lax.all_gather(parts, axes[k], axis=0, tiled=True)  28.2 us
    all_gather x1, waiting for transfers between devices, shards(): whole = lax.all_gather(tokens, 'tp', axis=1, tiled=True)  23.3 us
    all_gather x1, blocking collectives, stacked_from(): parts = lax.all_gather(parts, axes[k], axis=0, tiled=True)  13.1 us
  transfers between devices with their start and end apart: 6, of which 6 were waited for; matrix products, arithmetic and copies ran while one was open for 9% of the time, Pallas kernels for 0%

commit v1 on v0

v1 whole, which is shorter than its diff:
```python
import math

import jax
import jax.numpy as jnp
from jax import lax
from jax.sharding import Mesh
from jax.sharding import PartitionSpec as P

FSDP = ("z_hi", "y")
TP = ("z_lo", "x", "core")
SWAP = ((0, 0), (1, 2), (2, 1), (3, 3))


def dot(a, b, ca, cb):
    return lax.dot_general(a, b, (((ca,), (cb,)), ((), ())), preferred_element_type=jnp.float32)


def shards(tokens, out_grad, gate_weight, up_weight, down_weight):
    rows, width = tokens.shape
    factor = 1.0 / math.sqrt(rows * lax.axis_size(FSDP))
    both = jnp.stack([tokens, out_grad])
    both = lax.ppermute(both, ("z_hi", "z_lo"), SWAP)
    both = lax.all_gather(both, TP)
    n = both.shape[0] // 2
    both = both.reshape(2, n, 2, rows, width).transpose(2, 0, 3, 1, 4).reshape(2, 2 * rows, n * width)
    whole, grads = both[0], both[1]
    weights = jnp.stack([gate_weight, up_weight, down_weight.T])
    weights = lax.all_gather(weights, "y")
    weights = weights.transpose(1, 0, 2, 3).reshape(3, -1, gate_weight.shape[1])
    wg, wu, wd = weights[0], weights[1], weights[2]
    partial = jnp.stack([dot(whole, wg, 1, 0), dot(whole, wu, 1, 0), dot(grads, wd, 1, 0)])
    partial = partial.reshape(3, 2, rows, -1).transpose(1, 0, 2, 3)
    gate, up, hidden_grad = lax.psum_scatter(partial, "z_hi", scatter_dimension=0, tiled=False)
    squashed = jax.nn.sigmoid(gate)
    activated = gate * squashed
    slope = squashed * (1.0 + gate * (1.0 - squashed))
    hidden = (activated * up).astype(jnp.bfloat16)
    gate_delta = (hidden_grad * up * slope).astype(jnp.bfloat16)
    up_delta = (hidden_grad * activated).astype(jnp.bfloat16)
    acts = lax.all_gather(jnp.stack([gate_delta, up_delta, hidden]), "z_hi")
    acts = acts.transpose(1, 0, 2, 3).reshape(3, 2 * rows, -1)
    gd, ud, hid = acts[0], acts[1], acts[2]
    ig = dot(gd, wg, 1, 1) + dot(ud, wu, 1, 1)
    ig = ig.reshape(2, rows, n, width).transpose(0, 2, 1, 3).reshape(2 * n, rows, width)
    ig = lax.psum_scatter(ig, TP, scatter_dimension=0, tiled=False)
    input_grad = lax.ppermute(ig.astype(jnp.bfloat16), ("z_hi", "z_lo"), SWAP)
    joint = jnp.concatenate([dot(whole, gd, 0, 0), dot(whole, ud, 0, 0), dot(grads, hid, 0, 0)], axis=1) * factor
    summed = lax.psum_scatter(joint, "y", scatter_dimension=0, tiled=True)
    k = gd.shape[1]
    return (input_grad, summed[:, :k], summed[:, k : 2 * k], summed[:, 2 * k :].T)


def solution(mesh):
    finer = Mesh(mesh.devices.reshape(2, 4, 2, 4, 2), ("z_hi", "y", "z_lo", "x", "core"))
    return jax.shard_map(
        shards,
        mesh=finer,
        in_specs=(P(FSDP, TP), P(FSDP, TP), P(FSDP, TP), P(FSDP, TP), P(TP, FSDP)),
        out_specs=(P(FSDP, TP), P(FSDP, TP), P(FSDP, TP), P(TP, FSDP)),
        check_vma=False,
    )
```

time: 450 us -> 376 us (0.84)
  waiting for transfers between devices: 368 us -> 261 us
  local copies, waits for them, and re-layouts: 25.4 us -> 67.7 us
  matrix products: 20.7 us -> 13.9 us
  blocking collectives: 13.1 us -> 7.66 us
    reduce_scatter x2, waiting for transfers between devices: 212 us -> 126 us  [the longest x1 66.4 us: shards(): summed = lax.psum_scatter(joint, 'y', scatter_dimension=0, tiled=True)]
    all_gather x4 -> x2, waiting for transfers between devices: 154 us -> 92.6 us  [the longest x1 52.8 us: shards(): both = lax.all_gather(both, TP)]
    unnamed x6, waiting for transfers between devices: 1.27 us -> 42.3 us
    unnamed x11 -> x18, local copies, waits for them, and re-layouts: 4.28 us -> 20.1 us
    reshape x0 -> x1, local copies, waits for them, and re-layouts: none -> 11.4 us  [shards(): both.reshape(2, n, 2, rows, width).transpose(2, 0, 3, 1, 4)]
    another operation x2, local copies, waits for them, and re-layouts: 4.83 us -> 14.8 us  [laid_out(): parts.reshape(*dims[:dim], dims[dim] * dims[dim + 1], *dims[dim + 2:])]
    dot_general x8, matrix products: 20.7 us -> 13.9 us  [dot(): lax.dot_general(a, b, (((ca,), (cb,)), ((), ())), preferred_element_type=...]
    concatenate x2 -> x0, other arithmetic: 6.84 us -> none  [the longest x1 4.98 us: joint_term(): jnp.concatenate([column_term(whole, gate_delta, start, count, factor), co...]
  transfers between devices with their start and end apart: 6 -> 7, of which waited for: 6 -> 5; matrix products, arithmetic and copies ran while one was open for 9% -> 6% of each run, Pallas kernels for 0% -> 0%
where the time goes in v1:
time: 376 us
  waiting for transfers between devices  261 us (69%)
  local copies, waits for them, and re-layouts  67.7 us (18%)
  between operations  14 us (4%)
  matrix products  13.9 us (4%)
  other arithmetic  9.87 us (3%)
  blocking collectives  7.66 us (2%)
    reduce_scatter x1, waiting for transfers between devices, shards(): summed = lax.psum_scatter(joint, 'y', scatter_dimension=0, tiled=True)  66.4 us
    reduce_scatter x1, waiting for transfers between devices, shards(): ig = lax.psum_scatter(ig, TP, scatter_dimension=0, tiled=False)  59.7 us
    all_gather x1, waiting for transfers between devices, shards(): both = lax.all_gather(both, TP)  52.8 us
    unnamed x6, waiting for transfers between devices  42.3 us
    all_gather x1, waiting for transfers between devices, shards(): weights = lax.all_gather(weights, 'y')  39.8 us
    unnamed x18, local copies, waits for them, and re-layouts  20.1 us
    another operation x2, local copies, waits for them, and re-layouts  14.8 us
    dot_general x8, matrix products, dot(): lax.dot_general(a, b, (((ca,), (cb,)), ((), ())), preferred_element_type=...  13.9 us
  transfers between devices with their start and end apart: 7, of which 5 were waited for; matrix products, arithmetic and copies ran while one was open for 6% of the time, Pallas kernels for 0%

profile of v1, /device:TPU:1, one launch (start us, length us, event | category | flops | bytes accessed | tf_op | source)
XLA Modules:
  0.0 375.6 jit_solution(1829320640387958051)
XLA Ops:
  7.2 1.1 copy.19
  8.3 2.0 pad_maximum_fusion
  10.4 1.1 pad_maximum_fusion.1
  13.1 39.8 %all-gather.8.cloned.1.call-done = bf16[12,1024,128]{2,1,0:T(8,128)(2,1)} async-done(((bf16[3,1024,128]{2,1,0:T(8,128)(2,1)}), bf16[12,1024,128]{2,1,0:T(8,128)(2,1)}) %all-gather.8.cloned.1.call-update) | async-done | bytes 3145744 | tf_op jit(solution)/shard_map/all_gather | solution.py:28
  52.9 2.1 copy.34
  55.2 52.8 %all-gather.6.cloned.1.call-done = bf16[32,256,512]{2,1,0:T(8,128)(2,1)} async-done(((bf16[2,256,512]{2,1,0:T(8,128)(2,1)}), bf16[32,256,512]{2,1,0:T(8,128)(2,1)}) %all-gather.6.cloned.1.call-update) | async-done | bytes 8388624 | tf_op jit(solution)/shard_map/all_gather | solution.py:23
  108.0 11.4 %copy.33 = bf16[2,8,2,256,512]{4,1,3,0,2:T(8,128)(2,1)} copy(bf16[2,8,2,256,512]{4,3,2,1,0:T(8,128)(2,1)} %bitcast.122) | data formatting | bytes 16777216 | tf_op jit(solution)/shard_map/reshape | solution.py:25
  119.4 5.7 %fusion.1 = (bf16[1,2,256,8,512]{4,3,2,1,0:T(8,128)(2,1)}, bf16[1,2,256,8,512]{4,3,2,1,0:T(8,128)(2,1)}) fusion(bf16[2,2,256,8,512]{4,3,2,1,0:T(8,128)(2,1)} %bitcast.113), kind=kLoop, calls=%fused_computation.23 | loop fusion | bytes 16777216 | tf_op jit(solution)/shard_map/slice | solution.py:26
  125.2 7.4 %reshape.176 = bf16[2,256,4096]{2,1,0:T(8,128)(2,1)} reshape(bf16[1,2,256,8,512]{4,3,2,1,0:T(8,128)(2,1)} %get-tuple-element.12) | data formatting | bytes 8388608 | tf_op jit(solution)/shard_map/reshape.83
  132.6 3.6 convolution_bitcast_fusion.1
  136.2 2.0 convolution_bitcast_fusion.2
  138.1 7.4 %reshape.177 = bf16[2,256,4096]{2,1,0:T(8,128)(2,1)} reshape(bf16[1,2,256,8,512]{4,3,2,1,0:T(8,128)(2,1)} %get-tuple-element.13) | data formatting | bytes 8388608 | tf_op jit(solution)/shard_map/reshape.89
  145.5 3.5 convolution_bitcast_fusion
  149.0 1.0 maximum_bitcast_fusion
  150.6 42.2 %all-reduce.3.cloned.1.call-done = f32[2,3,256,128]{3,2,0,1:T(8,128)} async-done(((f32[2,3,256,128]{3,2,0,1:T(8,128)}), f32[2,3,256,128]{3,2,0,1:T(8,128)}) %all-reduce.3.cloned.1.call-update) | async-done | bytes 786448
  192.9 1.7 dynamic-slice_bitcast_fusion
  194.5 1.6 multiply_convert_fusion.2
  196.2 7.7 %all-gather.2 = bf16[6,256,128]{2,1,0:T(8,128)(2,1)S(1)} all-gather(bf16[3,256,128]{2,1,0:T(8,128)(2,1)S(1)} %pad_maximum_fusion.2), channel_id=4, replica_groups=mesh['z_hi'=2,'y'=4,'z_lo'=2,'x'=4,'core'=2] {'z_hi'}, dimensions={0}, use_global_device_ids=true | all-gather | bytes 589824 | tf_op jit(solution)/shard_map/all_gather | solution.py:40
  203.9 1.3 fusion.4
  205.2 1.3 convolution_add_fusion
  206.4 8.1 %copy.28 = f32[64,8,8,512]{3,2,1,0:T(8,128)S(1)} copy(f32[64,8,8,512]{3,1,2,0:T(8,128)S(1)} %bitcast.114) | data formatting | bytes 16777216
  214.6 1.2 bitcast_bitcast_fusion
  215.8 8.1 %copy.23 = f32[2,8,256,512]{3,2,1,0:T(8,128)} copy(f32[2,8,256,512]{3,1,2,0:T(8,128)S(1)} %bitcast_bitcast_fusion) | data formatting | bytes 16777216 | tf_op jit(solution)/shard_map/transpose | solution.py:44
  223.9 4.6 %copy.29 = bf16[64,8,8,512]{3,1,2,0:T(8,128)(2,1)S(1)} copy(bf16[64,8,8,512]{3,2,1,0:T(8,128)(2,1)} %bitcast.111) | data formatting | bytes 8388608
  228.6 2.2 copy.30
  233.1 3.1 maximum_multiply_fusion
  236.2 59.7 %reduce-scatter.6.cloned.1.call-done = f32[1,256,512]{2,1,0:T(8,128)} async-done(((f32[16,256,512]{2,1,0:T(8,128)}), f32[1,256,512]{2,1,0:T(8,128)}) %reduce-scatter.6.cloned.1.call-update) | async-done | bytes 524304 | tf_op jit(solution)/shard_map/reduce_scatter | solution.py:45
  295.9 1.1 convert_bitcast_fusion
  297.7 66.4 %reduce-scatter.8.cloned.1.call-done = f32[1024,384]{0,1:T(8,128)} async-done(((f32[4096,384]{0,1:T(8,128)}), f32[1024,384]{0,1:T(8,128)}) %reduce-scatter.8.cloned.1.call-update) | async-done | bytes 1572880 | tf_op jit(solution)/shard_map/reduce_scatter | solution.py:48
  364.1 2.3 slice_bitcast_fusion
  366.4 1.0 copy.24
  367.4 1.0 copy.25
  (32 shorter events, 6.3 us)
Async XLA Ops:
  7.2 45.7 %all-gather.8.cloned.1.call-start = ((), (), s32[]{:S(2)}) async-start(), calls=%async_computation.5 | async-start | bytes 3932160 | tf_op jit(solution)/shard_map/all_gather | solution.py:28
  10.4 97.6 %all-gather.6.cloned.1.call-start = ((), (), s32[]{:S(2)}) async-start(), calls=%async_computation.4 | async-start | bytes 8912896 | tf_op jit(solution)/shard_map/all_gather | solution.py:23
  11.5 0.7 collective-permute-start
  12.2 0.8 copy-start.3
  13.0 179.8 %all-reduce.3.cloned.1.call-start = ((), (), s32[]{:S(2)}) async-start(), calls=%async_computation.6 | async-start | bytes 1572864
  132.6 3.6 copy-start
  145.5 3.5 copy-start.2
  145.5 4.5 %copy-start.4 = (u32[128]{0:T(128)S(1)}, u32[128]{0:T(128)}, u32[]{:S(2)}) copy-start(u32[128]{0:T(128)} %constant.6) | copy-start | bytes 1540
  150.0 145.9 %reduce-scatter.6.cloned.1.call-start = ((), (), s32[]{:S(2)}) async-start(), calls=%async_computation.2 | async-start | bytes 8912896 | tf_op jit(solution)/shard_map/reduce_scatter | solution.py:45
  223.9 140.2 %reduce-scatter.8.cloned.1.call-start = ((), (), s32[]{:S(2)}) async-start(), calls=%async_computation.3 | async-start | bytes 7864320 | tf_op jit(solution)/shard_map/reduce_scatter | solution.py:48
  223.9 4.6 %copy-start.1 = (bf16[1,2,256,8,512]{4,3,2,1,0:T(8,128)(2,1)S(1)}, bf16[1,2,256,8,512]{4,3,2,1,0:T(8,128)(2,1)}, u32[]{:S(2)}) copy-start(bf16[1,2,256,8,512]{4,3,2,1,0:T(8,128)(2,1)} %get-tuple-element.13) | copy-start | bytes 12582916
  297.0 71.4 %collective-permute-start.1 = (bf16[256,512]{1,0:T(8,128)(2,1)S(1)}, bf16[256,512]{1,0:T(8,128)(2,1)S(1)}, u32[]{:S(2)}, u32[]{:S(2)}) collective-permute-start(bf16[256,512]{1,0:T(8,128)(2,1)S(1)} %convert_bitcast_fusion), channel_id=1, source_target_pairs={{0,0},{8,64},{64,8},{72,72},{1,1},{9,65},{65,9},{73,73},{2,2},{10,... | collective-permute-start | bytes 786440 | tf_op jit(solution)/shard_map/ppermute | solution.py:46
Sparse Core Ops, SparseCore 0:
  10.5 42.3 all-gather.7
  55.1 52.7 all-gather.5
  150.1 42.6 all-reduce.2
  224.0 71.8 reduce-scatter.5
  298.2 65.8 reduce-scatter.7

commit v2 on v1

v2 whole, which is shorter than its diff:
```python
import functools
import math

import jax
import jax.numpy as jnp
from jax import lax
from jax.experimental import pallas as pl
from jax.experimental.pallas import tpu as pltpu
from jax.sharding import Mesh
from jax.sharding import PartitionSpec as P

FSDP = ("z_hi", "y")
TP = ("z_lo", "x", "core")
MESH = pl.DeviceIdType.MESH
BF = jnp.bfloat16
F32 = jnp.float32
NSEM = 160
ROUNDS = ((0, 0), (0, 1), (1, 1), (1, 0))


def dot(a, b, ca, cb):
    return lax.dot_general(a, b, (((ca,), (cb,)), ((), ())), preferred_element_type=F32)


def kernel(factor, tok, og, wg, wu, wd, ig_o, gg_o, ug_o, dg_o,
           own, xb, wgu, wdn, pgu, ph, pgur, phr, agu, ah, igp, sibr, farr, nearr, zr, igs, igr,
           ws, hs, gb, hb, gfr, hfr, gnr, hnr, lsem, ssem, rsem):
    R, C = tok.shape
    F = wg.shape[1]
    H = R // 2
    z_hi, y, z_lo, x, core = (lax.axis_index(a) for a in ("z_hi", "y", "z_lo", "x", "core"))
    inner = (z_hi - z_lo) * (z_hi - z_lo)
    is_inner, is_outer = inner == 1, inner == 0
    nx, ny = 4, 4
    xr, xl, xf = lax.rem(x + 1, nx), lax.rem(x + nx - 1, nx), lax.rem(x + 2, nx)
    yr, yl, yf = lax.rem(y + 1, ny), lax.rem(y + ny - 1, ny), lax.rem(y + 2, ny)
    oc = 1 - core
    t_of = (z_hi, 1 - z_hi)
    d_xr, d_xl = (z_hi, y, z_lo, xr, core), (z_hi, y, z_lo, xl, core)
    d_yr, d_yl = (z_hi, yr, z_lo, x, core), (z_hi, yl, z_lo, x, core)
    d_sib = (z_hi, y, z_lo, x, oc)
    d_zlo = (z_hi, y, 1 - z_lo, x, core)
    d_zhi = (1 - z_hi, y, z_lo, x, core)
    d_zz = (1 - z_hi, y, 1 - z_lo, x, core)
    d_zs = (z_lo, y, 1 - z_lo, x, core)
    partners = (d_xr, d_xl, d_yr, d_yl, d_sib, d_zlo, d_zhi, d_zz)

    ids = {}

    def sid(name):
        return ids.setdefault(name, len(ids))

    for k in range(8):
        sid(("z", k))
    pending = []

    def send(name, src, dst, dev, rs=None, wait_later=True):
        i = sid(name)
        c = pltpu.make_async_remote_copy(
            src_ref=src, dst_ref=dst, send_sem=ssem.at[i], recv_sem=rsem.at[i if rs is None else rs],
            device_id=dev, device_id_type=MESH)
        c.start()
        if wait_later:
            pending.append(c)
        return c

    def recv(name, dst):
        i = sid(name)
        pltpu.make_async_remote_copy(
            src_ref=dst, dst_ref=dst, send_sem=ssem.at[i], recv_sem=rsem.at[i],
            device_id=d_sib, device_id_type=MESH).wait_recv()

    def trow(t):
        return pl.ds(pl.multiple_of(t * R, R), R)

    def blk(a, xp, c, t):
        return xb.at[a, 2 * xp + c, trow(t), :]

    def chunk(a, xp, t, h):
        return xb.at[a, 2 * xp + core, pl.ds(pl.multiple_of(t * R + h * H, H), H), :]

    loads_w = [
        pltpu.make_async_copy(wg, wgu.at[y, :, pl.ds(0, F)], lsem.at[0]),
        pltpu.make_async_copy(wu, wgu.at[y, :, pl.ds(F, F)], lsem.at[1]),
        pltpu.make_async_copy(wd, wdn.at[y], lsem.at[2]),
    ]
    loads_t = [
        pltpu.make_async_copy(tok, own.at[0], lsem.at[3]),
        pltpu.make_async_copy(og, own.at[1], lsem.at[4]),
    ]
    for c in loads_t + loads_w:
        c.start()

    @pl.when(is_outer)
    def _():
        pltpu.make_async_copy(tok, blk(0, x, core, z_hi), lsem.at[5]).start()
        pltpu.make_async_copy(og, blk(1, x, core, z_hi), lsem.at[6]).start()

    barrier = pltpu.get_barrier_semaphore()
    for d in partners:
        pl.semaphore_signal(barrier, inc=1, device_id=d, device_id_type=MESH)
    pl.semaphore_wait(barrier, len(partners))

    for c in loads_t:
        c.wait()

    for a in range(2):
        for h in range(2):
            k = 2 * a + h
            send(("zs", k), own.at[a, pl.ds(h * H, H), :], chunk(a, x, z_hi, h), d_zs, rs=4 * inner + k)

    @pl.when(is_outer)
    def _():
        pltpu.make_async_copy(tok, blk(0, x, core, z_hi), lsem.at[5]).wait()
        pltpu.make_async_copy(og, blk(1, x, core, z_hi), lsem.at[6]).wait()

    for c in loads_w:
        c.wait()

    def wchunk(which, yp, h):
        if which == 0:
            return wgu.at[yp, pl.ds(h * C, C), :]
        return wdn.at[yp, pl.ds(h * (F // 2), F // 2), :]

    def ysend(w):
        for h in range(2):
            send(("y", w, 0, h), wchunk(w, y, h), wchunk(w, y, h), d_yr)
            send(("y", w, 1, h), wchunk(w, y, h), wchunk(w, y, h), d_yl)

    def yfwd(w):
        recv(("y", w, 0, 0), wchunk(w, yl, 0))
        send(("yf", w, 0), wchunk(w, yl, 0), wchunk(w, yl, 0), d_yr)
        recv(("y", w, 1, 1), wchunk(w, yr, 1))
        send(("yf", w, 1), wchunk(w, yr, 1), wchunk(w, yr, 1), d_yl)

    def yfin(w):
        recv(("y", w, 0, 1), wchunk(w, yl, 1))
        recv(("y", w, 1, 0), wchunk(w, yr, 0))
        recv(("yf", w, 0), wchunk(w, yf, 0))
        recv(("yf", w, 1), wchunk(w, yf, 1))

    def xsend(r):
        a, rel = ROUNDS[r]
        t = t_of[rel]
        for h in range(2):
            k = 2 * a + h
            if rel == 0:
                @pl.when(is_inner)
                def _():
                    recv(("z", k), chunk(a, x, t, h))
            else:
                recv(("z", 4 + k), chunk(a, x, t, h))

                @pl.when(is_inner)
                def _():
                    send(("zr", k), chunk(a, x, t, h), chunk(a, x, t, h), d_zlo,
                         rs=4 + k, wait_later=False)
            send(("x", r, 0, h), chunk(a, x, t, h), chunk(a, x, t, h), d_xr)
            send(("x", r, 1, h), chunk(a, x, t, h), chunk(a, x, t, h), d_xl)
        send(("s", r, 0), blk(a, x, core, t), blk(a, x, core, t), d_sib)

    def xfwd(r):
        a, rel = ROUNDS[r]
        t = t_of[rel]
        recv(("x", r, 0, 0), chunk(a, xl, t, 0))
        send(("xf", r, 0), chunk(a, xl, t, 0), chunk(a, xl, t, 0), d_xr)
        recv(("x", r, 1, 1), chunk(a, xr, t, 1))
        send(("xf", r, 1), chunk(a, xr, t, 1), chunk(a, xr, t, 1), d_xl)

    def xfin(r):
        a, rel = ROUNDS[r]
        t = t_of[rel]
        recv(("x", r, 0, 1), chunk(a, xl, t, 1))
        send(("s", r, 1), blk(a, xl, core, t), blk(a, xl, core, t), d_sib)
        recv(("x", r, 1, 0), chunk(a, xr, t, 0))
        send(("s", r, 2), blk(a, xr, core, t), blk(a, xr, core, t), d_sib)
        recv(("xf", r, 0), chunk(a, xf, t, 0))
        recv(("xf", r, 1), chunk(a, xf, t, 1))
        send(("s", r, 3), blk(a, xf, core, t), blk(a, xf, core, t), d_sib)

    def sfin(r):
        a, rel = ROUNDS[r]
        t = t_of[rel]
        for j, xp in enumerate((x, xl, xr, xf)):
            recv(("s", r, j), blk(a, xp, oc, t))

    def half(e):
        return pl.ds(pl.multiple_of(lax.rem(e, 2) * C, C), C)

    def forward(r):
        a, rel = ROUNDS[r]
        t = t_of[rel]
        out = (pgu, ph)[a].at[rel]
        out[...] = jnp.zeros(out.shape, F32)

        def step(e, carry):
            block = xb[a, e, trow(t), :]
            if a == 0:
                out[...] += dot(block, wgu[e // 2, half(e), :], 1, 0)
            else:
                out[...] += dot(block, wdn[e // 2, :, half(e)], 1, 1)
            return carry

        lax.fori_loop(0, 2 * nx, step, 0)

    ysend(0)
    xsend(0)
    xfwd(0)
    xsend(1)
    yfwd(0)
    ysend(1)
    xfin(0)
    xfwd(1)
    xsend(2)
    xfin(1)
    xfwd(2)
    xsend(3)
    yfwd(1)
    yfin(0)
    sfin(0)
    sfin(1)
    forward(1)
    send("pgu", pgu.at[1], pgur, d_zhi)
    forward(0)
    xfin(2)
    xfwd(3)
    yfin(1)
    sfin(2)
    forward(2)
    send("ph", ph.at[1], phr, d_zhi)
    xfin(3)
    sfin(3)
    forward(3)

    recv("pgu", pgur)
    recv("ph", phr)
    gate = pgu[0, :, :F] + pgur[:, :F]
    up = pgu[0, :, F:] + pgur[:, F:]
    hg = ph[0] + phr[...]
    squashed = jax.nn.sigmoid(gate)
    activated = gate * squashed
    slope = squashed * (1.0 + gate * (1.0 - squashed))
    agu[trow(z_hi), :F] = (hg * up * slope).astype(BF)
    agu[trow(z_hi), F:] = (hg * activated).astype(BF)
    ah[trow(z_hi), :] = (activated * up).astype(BF)
    send("agu", agu.at[trow(z_hi), :], agu.at[trow(z_hi), :], d_zhi)
    send("ah", ah.at[trow(z_hi), :], ah.at[trow(z_hi), :], d_zhi)

    order = (xf, xr, xl, x)

    def igstart(rel):
        def step(e, carry):
            igp[rel, e] = dot(agu[trow(t_of[rel]), :], wgu[e // 2, half(e), :], 1, 1)
            return carry

        lax.fori_loop(0, 2 * nx, step, 0)
        for j, xp in enumerate(order):
            send(("is", rel, j), igp.at[rel, 2 * xp + oc], sibr.at[rel, xp], d_sib)

    def addsib(rel, j):
        xp = order[j]
        recv(("is", rel, j), sibr.at[rel, xp])
        igp[rel, 2 * xp + core] += sibr[rel, xp]

    def hrow(h):
        return pl.ds(h * H, H)

    def igfirst(rel):
        addsib(rel, 0)
        for h, d in enumerate((d_xr, d_xl)):
            send(("if", rel, h), igp.at[rel, 2 * xf + core, hrow(h), :], farr.at[rel, h], d)
        for h, (j, xp, d) in enumerate(((1, xr, d_xr), (2, xl, d_xl))):
            addsib(rel, j)
            send(("in", rel, h, 1 - h), igp.at[rel, 2 * xp + core, hrow(1 - h), :],
                 nearr.at[rel, h, hrow(1 - h), :], d)

    def igsecond(rel):
        for h, (xp, d) in enumerate(((xr, d_xr), (xl, d_xl))):
            recv(("if", rel, h), farr.at[rel, h])
            igp[rel, 2 * xp + core, hrow(h), :] += farr[rel, h]
            send(("in", rel, h, h), igp.at[rel, 2 * xp + core, hrow(h), :], nearr.at[rel, h, hrow(h), :], d)
        addsib(rel, 3)

    def iglast(rel):
        for h in range(2):
            for g in range(2):
                recv(("in", rel, h, g), nearr.at[rel, h, hrow(g), :])
        igp[rel, 2 * x + core] += nearr[rel, 0] + nearr[rel, 1]

    igstart(0)
    igfirst(0)
    recv("agu", agu.at[trow(1 - z_hi), :])
    recv("ah", ah.at[trow(1 - z_hi), :])
    igstart(1)
    igfirst(1)

    def wstep(e, carry):
        g = dot(xb[0, e], agu[...], 0, 0)
        ws[e] = g
        gb[e] = g.astype(BF)
        d = dot(ah[...], xb[1, e], 0, 0)
        hs[e] = d
        hb[e] = d.astype(BF)
        return carry

    lax.fori_loop(0, 2 * ny, wstep, 0)
    sides = ((yr, d_yr), (yl, d_yl))
    for h, (yp, d) in enumerate(sides):
        send(("gf", h), gb.at[2 * yf + h], gfr.at[h], d)
        send(("hf", h), hb.at[2 * yf + h], hfr.at[h], d)
    for h, (yp, d) in enumerate(sides):
        send(("gn", h, 1 - h), gb.at[2 * yp + 1 - h], gnr.at[h, 1 - h], d)
        send(("hn", h, 1 - h), hb.at[2 * yp + 1 - h], hnr.at[h, 1 - h], d)

    igsecond(1)
    igsecond(0)

    for h, (yp, d) in enumerate(sides):
        recv(("gf", h), gfr.at[h])
        gb[2 * yp + h] = (ws[2 * yp + h] + gfr[h].astype(F32)).astype(BF)
        send(("gn", h, h), gb.at[2 * yp + h], gnr.at[h, h], d)
        recv(("hf", h), hfr.at[h])
        hb[2 * yp + h] = (hs[2 * yp + h] + hfr[h].astype(F32)).astype(BF)
        send(("hn", h, h), hb.at[2 * yp + h], hnr.at[h, h], d)

    def zsend(rel):
        for h in range(2):
            send(("zi", rel, h), igp.at[rel, 2 * x + core, hrow(h), :], zr.at[hrow(h), :], d_zlo,
                 rs=sid(("zir", h)), wait_later=False)

    iglast(1)

    @pl.when(is_outer)
    def _():
        zsend(1)

    iglast(0)

    @pl.when(is_inner)
    def _():
        zsend(0)

    @pl.when(is_inner)
    def _():
        for h in range(2):
            recv(("zir", h), zr.at[hrow(h), :])
            igs[hrow(h), :] = (igp[1, 2 * x + core, hrow(h), :] + zr[hrow(h), :]).astype(BF)
            send(("zo", h), igs.at[hrow(h), :], igr.at[hrow(h), :], d_zz, wait_later=False)

    for h in range(2):
        for s in range(2):
            recv(("gn", s, h), gnr.at[s, h])
            recv(("hn", s, h), hnr.at[s, h])
        g = (ws[2 * y + h] + gnr[0, h].astype(F32) + gnr[1, h].astype(F32)) * factor
        gg_o[pl.ds(h * C, C), :] = g[:, :F]
        ug_o[pl.ds(h * C, C), :] = g[:, F:]
        dg_o[:, pl.ds(h * C, C)] = (hs[2 * y + h] + hnr[0, h].astype(F32) + hnr[1, h].astype(F32)) * factor

    @pl.when(is_outer)
    def _():
        for h in range(2):
            recv(("zir", h), zr.at[hrow(h), :])
            ig_o[hrow(h), :] = (igp[0, 2 * x + core, hrow(h), :] + zr[hrow(h), :]).astype(BF)

    def wait_send(name, src):
        i = sid(name)
        pltpu.make_async_remote_copy(
            src_ref=src, dst_ref=src, send_sem=ssem.at[i], recv_sem=rsem.at[i],
            device_id=d_sib, device_id_type=MESH).wait_send()

    @pl.when(is_inner)
    def _():
        for h in range(2):
            recv(("zo", h), igr.at[hrow(h), :])
        ig_o[...] = igr[...]
        for h in range(2):
            wait_send(("zo", h), igs.at[hrow(h), :])
            wait_send(("zi", 0, h), zr.at[hrow(h), :])
        for k in range(4):
            wait_send(("zr", k), own.at[k // 2, hrow(k % 2), :])

    @pl.when(is_outer)
    def _():
        for h in range(2):
            wait_send(("zi", 1, h), zr.at[hrow(h), :])

    for c in pending:
        c.wait_send()
    assert len(ids) <= NSEM


def shards(tokens, out_grad, gate_weight, up_weight, down_weight):
    R, C = tokens.shape
    F = gate_weight.shape[1]
    H = R // 2
    factor = 1.0 / math.sqrt(R * lax.axis_size(FSDP))
    anyspec = pl.BlockSpec(memory_space=pl.ANY)
    vm = pl.BlockSpec(memory_space=pltpu.VMEM)
    V = pltpu.VMEM
    scratch = [
        V((2, R, C), BF), V((2, 8, 2 * R, C), BF), V((4, 2 * C, 2 * F), BF), V((4, F, 2 * C), BF),
        V((2, R, 2 * F), F32), V((2, R, F), F32), V((R, 2 * F), F32), V((R, F), F32),
        V((2 * R, 2 * F), BF), V((2 * R, F), BF),
        V((2, 8, R, C), F32), V((2, 4, R, C), F32), V((2, 2, H, C), F32), V((2, 2, R, C), F32),
        V((R, C), F32), V((R, C), BF), V((R, C), BF),
        V((8, C, 2 * F), F32), V((8, F, C), F32), V((8, C, 2 * F), BF), V((8, F, C), BF),
        V((2, C, 2 * F), BF), V((2, F, C), BF), V((2, 2, C, 2 * F), BF), V((2, 2, F, C), BF),
        pltpu.SemaphoreType.DMA((8,)), pltpu.SemaphoreType.DMA((NSEM,)), pltpu.SemaphoreType.DMA((NSEM,)),
    ]
    return pl.pallas_call(
        functools.partial(kernel, factor),
        out_shape=(
            jax.ShapeDtypeStruct((R, C), BF),
            jax.ShapeDtypeStruct((2 * C, F), F32),
            jax.ShapeDtypeStruct((2 * C, F), F32),
            jax.ShapeDtypeStruct((F, 2 * C), F32),
        ),
        in_specs=[anyspec] * 5,
        out_specs=(vm,) * 4,
        scratch_shapes=scratch,
        compiler_params=pltpu.CompilerParams(
            collective_id=0, has_side_effects=True, vmem_limit_bytes=60 * 1024 * 1024),
        name="ffn_backward",
    )(tokens, out_grad, gate_weight, up_weight, down_weight)


def solution(mesh):
    finer = Mesh(mesh.devices.reshape(2, 4, 2, 4, 2), ("z_hi", "y", "z_lo", "x", "core"))
    return jax.shard_map(
        shards,
        mesh=finer,
        in_specs=(P(FSDP, TP), P(FSDP, TP), P(FSDP, TP), P(FSDP, TP), P(TP, FSDP)),
        out_specs=(P(FSDP, TP), P(FSDP, TP), P(FSDP, TP), P(TP, FSDP)),
        check_vma=False,
    )
```

time: 376 us -> 116 us (0.31)
  waiting for transfers between devices: 261 us -> 0 us
  Pallas kernels: 0 us -> 110 us
  local copies, waits for them, and re-layouts: 67.7 us -> 4.98 us
  matrix products: 13.9 us -> 0 us
  between operations: 14 us -> 0.65 us
  other arithmetic: 9.87 us -> 0 us
  blocking collectives: 7.66 us -> 0 us
    reduce_scatter x2 -> x0, waiting for transfers between devices: 126 us -> none  [the longest x1 66.4 us: shards(): summed = lax.psum_scatter(joint, 'y', scatter_dimension=0, tiled=True)]
    pallas_call x0 -> x1, Pallas kernels: none -> 110 us  [shards(): pl.pallas_call(functools.partial(kernel, factor), out_shape=(jax.ShapeDty...]
    all_gather x2 -> x0, waiting for transfers between devices: 92.6 us -> none  [the longest x1 52.8 us: shards(): both = lax.all_gather(both, TP)]
    unnamed x6 -> x0, waiting for transfers between devices: 42.3 us -> none
    unnamed x18 -> x10, local copies, waits for them, and re-layouts: 20.1 us -> 4.98 us
    another operation x2 -> x0, local copies, waits for them, and re-layouts: 14.8 us -> none
    dot_general x8 -> x0, matrix products: 13.9 us -> none  [dot(): lax.dot_general(a, b, (((ca,), (cb,)), ((), ())), preferred_element_type=...]
    transpose x3 -> x0, local copies, waits for them, and re-layouts: 11.6 us -> none  [the longest x2 9.3 us: shards(): ig.reshape(2, rows, n, width).transpose(0, 2, 1, 3)]
  transfers between devices with their start and end apart: 7 -> 0, of which waited for: 5 -> 0; matrix products, arithmetic and copies ran while one was open for 6% -> 0% of each run, Pallas kernels for 0% -> 0%
where the time goes in v2:
time: 116 us
  Pallas kernels  110 us (95%)
  local copies, waits for them, and re-layouts  4.98 us (4%)
    pallas_call x1, Pallas kernels, shards(): pl.pallas_call(functools.partial(kernel, factor), out_shape=(jax.ShapeDty...  110 us
    unnamed x10, local copies, waits for them, and re-layouts  4.98 us

profile of v2, /device:TPU:1, one launch (start us, length us, event | category | flops | bytes accessed | tf_op | source)
XLA Modules:
  0.0 116.0 jit_solution(8005248262453265476)
XLA Ops:
  0.6 110.4 %ffn_backward.1 = (bf16[256,512]{1,0:T(8,128)(2,1)}, f32[1024,128]{1,0:T(8,128)}, f32[1024,128]{1,0:T(8,128)}, f32[128,1024]{1,0:T(8,128)}) custom-call(bf16[256,512]{1,0:T(8,128)(2,1)} %tok.1, bf16[256,512]{1,0:T(8,128)(2,1)} %og.1, bf16[1024,128]{1,0:T(8,128)(2,1)} %wg.1, bf16[1024,128]{1,0:T(8,128)(2,1)} %wu.1, bf16[128,1024]{1,0:T(8,128)(2,1)} %wd.1), custom_call_target="tpu_custom_call" | custom-call | tf_op jit(solution)/shard_map/ffn_backward/pallas_call | solution.py:410
  111.0 0.0 copy-start.2
  111.0 1.7 %copy.13 = bf16[256,512]{1,0:T(8,128)(2,1)} copy(bf16[256,512]{1,0:T(8,128)(2,1)} %get-tuple-element.8) | data formatting | bytes 524288
  112.7 0.0 copy-done.2
  112.7 0.0 copy-start.1
  112.7 0.8 copy.14
  113.5 0.4 copy-done.1
  114.0 0.0 copy-start
  114.0 0.8 copy.15
  114.8 0.4 copy-done
  115.2 0.8 copy.16
Async XLA Ops:
  111.0 1.7 %copy-start.2 = (f32[1024,128]{1,0:T(8,128)S(1)}, f32[1024,128]{1,0:T(8,128)}, u32[]{:S(2)}) copy-start(f32[1024,128]{1,0:T(8,128)} %get-tuple-element.9) | copy-start | bytes 1572868
  112.7 1.2 %copy-start.1 = (f32[1024,128]{1,0:T(8,128)S(1)}, f32[1024,128]{1,0:T(8,128)}, u32[]{:S(2)}) copy-start(f32[1024,128]{1,0:T(8,128)} %get-tuple-element.10) | copy-start | bytes 1572868
  114.0 1.2 %copy-start = (f32[128,1024]{1,0:T(8,128)S(1)}, f32[128,1024]{1,0:T(8,128)}, u32[]{:S(2)}) copy-start(f32[128,1024]{1,0:T(8,128)} %get-tuple-element.11) | copy-start | bytes 1572868

commit v3 on v2

--- a/solution.py
+++ b/solution.py
@@ -14,8 +14,9 @@
 MESH = pl.DeviceIdType.MESH
 BF = jnp.bfloat16
 F32 = jnp.float32
-NSEM = 160
-ROUNDS = ((0, 0), (0, 1), (1, 1), (1, 0))
+NSEM = 192
+HOME = 128
+ROUNDS = ((0, 0, HOME, 256 - HOME), (0, 1, HOME, 256 - HOME), (1, 1, 0, 256), (1, 0, 0, 256))
 
 
 def dot(a, b, ca, cb):
@@ -23,7 +24,7 @@
 
 
 def kernel(factor, tok, og, wg, wu, wd, ig_o, gg_o, ug_o, dg_o,
-           own, xb, wgu, wdn, pgu, ph, pgur, phr, agu, ah, igp, sibr, farr, nearr, zr, igs, igr,
+           own, xb, wgu, wdn, pgu, ph, pgur, phr, agu, ah, igp, sibr, farr, nearr, fs, zr, igs, igr,
            ws, hs, gb, hb, gfr, hfr, gnr, hnr, lsem, ssem, rsem):
     R, C = tok.shape
     F = wg.shape[1]
@@ -52,6 +53,8 @@
 
     for k in range(8):
         sid(("z", k))
+    for k in range(8):
+        sid(("zh", k))
     pending = []
 
     def send(name, src, dst, dev, rs=None, wait_later=True):
@@ -76,8 +79,21 @@
     def blk(a, xp, c, t):
         return xb.at[a, 2 * xp + c, trow(t), :]
 
-    def chunk(a, xp, t, h):
-        return xb.at[a, 2 * xp + core, pl.ds(pl.multiple_of(t * R + h * H, H), H), :]
+    def rows(start, n):
+        return pl.ds(pl.multiple_of(start, 16), n)
+
+    def chunk(a, xp, t, h, r0, n):
+        return xb.at[a, 2 * xp + core, rows(t * R + r0 + h * (n // 2), n // 2), :]
+
+    def part(a, xp, c, t, r0, n):
+        return xb.at[a, 2 * xp + c, rows(t * R + r0, n), :]
+
+    home_at = (1 - inner) * z_hi * R + inner * 2 * R
+
+    def home(xp, h=None):
+        if h is None:
+            return xb.at[0, 2 * xp + core, rows(home_at, HOME), :]
+        return xb.at[0, 2 * xp + core, rows(home_at + h * (HOME // 2), HOME // 2), :]
 
     loads_w = [
         pltpu.make_async_copy(wg, wgu.at[y, :, pl.ds(0, F)], lsem.at[0]),
@@ -91,10 +107,17 @@
     for c in loads_t + loads_w:
         c.start()
 
+    outer_loads = (
+        (tok.at[pl.ds(HOME, R - HOME), :], part(0, x, core, z_hi, HOME, R - HOME), lsem.at[5]),
+        (og, blk(1, x, core, z_hi), lsem.at[6]),
+    )
+    load_home = pltpu.make_async_copy(tok.at[pl.ds(0, HOME), :], home(x), lsem.at[7])
+    load_home.start()
+
     @pl.when(is_outer)
     def _():
-        pltpu.make_async_copy(tok, blk(0, x, core, z_hi), lsem.at[5]).start()
-        pltpu.make_async_copy(og, blk(1, x, core, z_hi), lsem.at[6]).start()
+        for c in outer_loads:
+            pltpu.make_async_copy(*c).start()
 
     barrier = pltpu.get_barrier_semaphore()
     for d in partners:
@@ -103,16 +126,18 @@
 
     for c in loads_t:
         c.wait()
-
-    for a in range(2):
+    load_home.wait()
+
+    for a, rel, r0, n in (ROUNDS[0], ROUNDS[3]):
         for h in range(2):
             k = 2 * a + h
-            send(("zs", k), own.at[a, pl.ds(h * H, H), :], chunk(a, x, z_hi, h), d_zs, rs=4 * inner + k)
+            send(("zs", k), own.at[a, pl.ds(r0 + h * (n // 2), n // 2), :], chunk(a, x, z_hi, h, r0, n), d_zs,
+                 rs=4 * inner + k)
 
     @pl.when(is_outer)
     def _():
-        pltpu.make_async_copy(tok, blk(0, x, core, z_hi), lsem.at[5]).wait()
-        pltpu.make_async_copy(og, blk(1, x, core, z_hi), lsem.at[6]).wait()
+        for c in outer_loads:
+            pltpu.make_async_copy(*c).wait()
 
     for c in loads_w:
         c.wait()
@@ -139,56 +164,117 @@
         recv(("yf", w, 0), wchunk(w, yf, 0))
         recv(("yf", w, 1), wchunk(w, yf, 1))
 
-    def xsend(r):
-        a, rel = ROUNDS[r]
+    def hsend():
+        for h in range(2):
+            send(("h", 0, h), home(x, h), home(x, h), d_xr)
+            send(("h", 1, h), home(x, h), home(x, h), d_xl)
+
+    def homez(j, xp):
+        send(("hz", j), home(xp), xb.at[0, 2 * xp + core, rows(z_hi * R, HOME), :], d_zs, rs=8 + 4 * inner + j)
+
+    def hfwd():
+        recv(("h", 0, 0), home(xl, 0))
+        send(("hf", 0), home(xl, 0), home(xl, 0), d_xr)
+        recv(("h", 1, 1), home(xr, 1))
+        send(("hf", 1), home(xr, 1), home(xr, 1), d_xl)
+
+    def hfin():
+        homez(0, x)
+        recv(("h", 0, 1), home(xl, 1))
+        homez(1, xl)
+        recv(("h", 1, 0), home(xr, 0))
+        homez(2, xr)
+        recv(("hf", 0), home(xf, 0))
+        recv(("hf", 1), home(xf, 1))
+        homez(3, xf)
+
+    xorder = (x, xl, xr, xf)
+
+    def hz(rel):
         t = t_of[rel]
-        for h in range(2):
-            k = 2 * a + h
+        for j, xp in enumerate(xorder):
+            p = part(0, xp, core, t, 0, HOME)
             if rel == 0:
                 @pl.when(is_inner)
                 def _():
-                    recv(("z", k), chunk(a, x, t, h))
+                    recv(("zh", j), p)
             else:
-                recv(("z", 4 + k), chunk(a, x, t, h))
+                recv(("zh", 4 + j), p)
 
                 @pl.when(is_inner)
                 def _():
-                    send(("zr", k), chunk(a, x, t, h), chunk(a, x, t, h), d_zlo,
-                         rs=4 + k, wait_later=False)
-            send(("x", r, 0, h), chunk(a, x, t, h), chunk(a, x, t, h), d_xr)
-            send(("x", r, 1, h), chunk(a, x, t, h), chunk(a, x, t, h), d_xl)
-        send(("s", r, 0), blk(a, x, core, t), blk(a, x, core, t), d_sib)
+                    send(("hzr", j), p, p, d_zlo, rs=12 + j, wait_later=False)
+            send(("hs", rel, j), p, p, d_sib)
+
+    def hsfin(rel):
+        for j, xp in enumerate(xorder):
+            recv(("hs", rel, j), part(0, xp, oc, t_of[rel], 0, HOME))
+
+    def relay(r):
+        a, rel, r0, n = ROUNDS[r]
+        t = t_of[rel]
+        for h in range(2):
+            k = 2 * a + h
+
+            @pl.when(is_inner)
+            def _():
+                c = chunk(a, x, t, h, r0, n)
+                recv(("z", 4 + k), c)
+                send(("zr", k), c, c, d_zlo, rs=4 + k, wait_later=False)
+
+    def xsend(r):
+        a, rel, r0, n = ROUNDS[r]
+        t = t_of[rel]
+        for h in range(2):
+            k = 2 * a + h
+            c = chunk(a, x, t, h, r0, n)
+            if rel == 0:
+                @pl.when(is_inner)
+                def _():
+                    recv(("z", k), c)
+            else:
+                @pl.when(is_outer)
+                def _():
+                    recv(("z", 4 + k), c)
+            send(("x", r, 0, h), c, c, d_xr)
+            send(("x", r, 1, h), c, c, d_xl)
+        p = part(a, x, core, t, r0, n)
+        send(("s", r, 0), p, p, d_sib)
 
     def xfwd(r):
-        a, rel = ROUNDS[r]
+        a, rel, r0, n = ROUNDS[r]
         t = t_of[rel]
-        recv(("x", r, 0, 0), chunk(a, xl, t, 0))
-        send(("xf", r, 0), chunk(a, xl, t, 0), chunk(a, xl, t, 0), d_xr)
-        recv(("x", r, 1, 1), chunk(a, xr, t, 1))
-        send(("xf", r, 1), chunk(a, xr, t, 1), chunk(a, xr, t, 1), d_xl)
+        c = chunk(a, xl, t, 0, r0, n)
+        recv(("x", r, 0, 0), c)
+        send(("xf", r, 0), c, c, d_xr)
+        c = chunk(a, xr, t, 1, r0, n)
+        recv(("x", r, 1, 1), c)
+        send(("xf", r, 1), c, c, d_xl)
 
     def xfin(r):
-        a, rel = ROUNDS[r]
+        a, rel, r0, n = ROUNDS[r]
         t = t_of[rel]
-        recv(("x", r, 0, 1), chunk(a, xl, t, 1))
-        send(("s", r, 1), blk(a, xl, core, t), blk(a, xl, core, t), d_sib)
-        recv(("x", r, 1, 0), chunk(a, xr, t, 0))
-        send(("s", r, 2), blk(a, xr, core, t), blk(a, xr, core, t), d_sib)
-        recv(("xf", r, 0), chunk(a, xf, t, 0))
-        recv(("xf", r, 1), chunk(a, xf, t, 1))
-        send(("s", r, 3), blk(a, xf, core, t), blk(a, xf, core, t), d_sib)
+        recv(("x", r, 0, 1), chunk(a, xl, t, 1, r0, n))
+        p = part(a, xl, core, t, r0, n)
+        send(("s", r, 1), p, p, d_sib)
+        recv(("x", r, 1, 0), chunk(a, xr, t, 0, r0, n))
+        p = part(a, xr, core, t, r0, n)
+        send(("s", r, 2), p, p, d_sib)
+        recv(("xf", r, 0), chunk(a, xf, t, 0, r0, n))
+        recv(("xf", r, 1), chunk(a, xf, t, 1, r0, n))
+        p = part(a, xf, core, t, r0, n)
+        send(("s", r, 3), p, p, d_sib)
 
     def sfin(r):
-        a, rel = ROUNDS[r]
-        t = t_of[rel]
-        for j, xp in enumerate((x, xl, xr, xf)):
-            recv(("s", r, j), blk(a, xp, oc, t))
+        a, rel, r0, n = ROUNDS[r]
+        for j, xp in enumerate(xorder):
+            recv(("s", r, j), part(a, xp, oc, t_of[rel], r0, n))
 
     def half(e):
         return pl.ds(pl.multiple_of(lax.rem(e, 2) * C, C), C)
 
     def forward(r):
-        a, rel = ROUNDS[r]
+        a, rel, r0, n = ROUNDS[r]
         t = t_of[rel]
         out = (pgu, ph)[a].at[rel]
         out[...] = jnp.zeros(out.shape, F32)
@@ -203,27 +289,36 @@
 
         lax.fori_loop(0, 2 * nx, step, 0)
 
+    hsend()
     ysend(0)
     xsend(0)
-    xfwd(0)
+    hfwd()
+    relay(1)
     xsend(1)
+    hfin()
+    relay(2)
     yfwd(0)
     ysend(1)
+    xfwd(0)
+    xsend(2)
     xfin(0)
     xfwd(1)
-    xsend(2)
+    xsend(3)
     xfin(1)
     xfwd(2)
-    xsend(3)
+    hz(0)
+    hz(1)
     yfwd(1)
     yfin(0)
     sfin(0)
     sfin(1)
+    xfin(2)
+    xfwd(3)
+    hsfin(0)
+    hsfin(1)
     forward(1)
     send("pgu", pgu.at[1], pgur, d_zhi)
     forward(0)
-    xfin(2)
-    xfwd(3)
     yfin(1)
     sfin(2)
     forward(2)
@@ -268,7 +363,8 @@
     def igfirst(rel):
         addsib(rel, 0)
         for h, d in enumerate((d_xr, d_xl)):
-            send(("if", rel, h), igp.at[rel, 2 * xf + core, hrow(h), :], farr.at[rel, h], d)
+            fs[rel, h] = igp[rel, 2 * xf + core, hrow(h), :].astype(BF)
+            send(("if", rel, h), fs.at[rel, h], farr.at[rel, h], d)
         for h, (j, xp, d) in enumerate(((1, xr, d_xr), (2, xl, d_xl))):
             addsib(rel, j)
             send(("in", rel, h, 1 - h), igp.at[rel, 2 * xp + core, hrow(1 - h), :],
@@ -277,7 +373,7 @@
     def igsecond(rel):
         for h, (xp, d) in enumerate(((xr, d_xr), (xl, d_xl))):
             recv(("if", rel, h), farr.at[rel, h])
-            igp[rel, 2 * xp + core, hrow(h), :] += farr[rel, h]
+            igp[rel, 2 * xp + core, hrow(h), :] += farr[rel, h].astype(F32)
             send(("in", rel, h, h), igp.at[rel, 2 * xp + core, hrow(h), :], nearr.at[rel, h, hrow(h), :], d)
         addsib(rel, 3)
 
@@ -295,10 +391,10 @@
     igfirst(1)
 
     def wstep(e, carry):
-        g = dot(xb[0, e], agu[...], 0, 0)
+        g = dot(xb[0, e, : 2 * R], agu[...], 0, 0)
         ws[e] = g
         gb[e] = g.astype(BF)
-        d = dot(ah[...], xb[1, e], 0, 0)
+        d = dot(ah[...], xb[1, e, : 2 * R], 0, 0)
         hs[e] = d
         hb[e] = d.astype(BF)
         return carry
@@ -376,8 +472,12 @@
         for h in range(2):
             wait_send(("zo", h), igs.at[hrow(h), :])
             wait_send(("zi", 0, h), zr.at[hrow(h), :])
-        for k in range(4):
-            wait_send(("zr", k), own.at[k // 2, hrow(k % 2), :])
+        for r in (1, 2):
+            a, rel, r0, n = ROUNDS[r]
+            for h in range(2):
+                wait_send(("zr", 2 * a + h), chunk(a, x, t_of[1], h, r0, n))
+        for j, xp in enumerate(xorder):
+            wait_send(("hzr", j), part(0, xp, core, t_of[1], 0, HOME))
 
     @pl.when(is_outer)
     def _():
@@ -398,10 +498,10 @@
     vm = pl.BlockSpec(memory_space=pltpu.VMEM)
     V = pltpu.VMEM
     scratch = [
-        V((2, R, C), BF), V((2, 8, 2 * R, C), BF), V((4, 2 * C, 2 * F), BF), V((4, F, 2 * C), BF),
+        V((2, R, C), BF), V((2, 8, 2 * R + HOME, C), BF), V((4, 2 * C, 2 * F), BF), V((4, F, 2 * C), BF),
         V((2, R, 2 * F), F32), V((2, R, F), F32), V((R, 2 * F), F32), V((R, F), F32),
         V((2 * R, 2 * F), BF), V((2 * R, F), BF),
-        V((2, 8, R, C), F32), V((2, 4, R, C), F32), V((2, 2, H, C), F32), V((2, 2, R, C), F32),
+        V((2, 8, R, C), F32), V((2, 4, R, C), F32), V((2, 2, H, C), BF), V((2, 2, R, C), F32), V((2, 2, H, C), BF),
         V((R, C), F32), V((R, C), BF), V((R, C), BF),
         V((8, C, 2 * F), F32), V((8, F, C), F32), V((8, C, 2 * F), BF), V((8, F, C), BF),
         V((2, C, 2 * F), BF), V((2, F, C), BF), V((2, 2, C, 2 * F), BF), V((2, 2, F, C), BF),

time: 116 us -> 111 us (0.957)
  Pallas kernels: 110 us -> 105 us
    pallas_call x1, Pallas kernels: 110 us -> 105 us  [shards(): pl.pallas_call(functools.partial(kernel, factor), out_shape=(jax.ShapeDty...]
where the time goes in v3:
time: 111 us
  Pallas kernels  105 us (95%)
  local copies, waits for them, and re-layouts  4.98 us (4%)
    pallas_call x1, Pallas kernels, shards(): pl.pallas_call(functools.partial(kernel, factor), out_shape=(jax.ShapeDty...  105 us
    unnamed x10, local copies, waits for them, and re-layouts  4.98 us

profile of v3, /device:TPU:1, one launch (start us, length us, event | category | flops | bytes accessed | tf_op | source)
XLA Modules:
  0.0 110.7 jit_solution(452579759666158837)
XLA Ops:
  0.6 105.1 %ffn_backward.1 = (bf16[256,512]{1,0:T(8,128)(2,1)}, f32[1024,128]{1,0:T(8,128)}, f32[1024,128]{1,0:T(8,128)}, f32[128,1024]{1,0:T(8,128)}) custom-call(bf16[256,512]{1,0:T(8,128)(2,1)} %tok.1, bf16[256,512]{1,0:T(8,128)(2,1)} %og.1, bf16[1024,128]{1,0:T(8,128)(2,1)} %wg.1, bf16[1024,128]{1,0:T(8,128)(2,1)} %wu.1, bf16[128,1024]{1,0:T(8,128)(2,1)} %wd.1), custom_call_target="tpu_custom_call" | custom-call | tf_op jit(solution)/shard_map/ffn_backward/pallas_call | solution.py:510
  105.7 0.0 copy-start.2
  105.7 1.7 %copy.13 = bf16[256,512]{1,0:T(8,128)(2,1)} copy(bf16[256,512]{1,0:T(8,128)(2,1)} %get-tuple-element.8) | data formatting | bytes 524288
  107.4 0.0 copy-done.2
  107.4 0.0 copy-start.1
  107.4 0.8 copy.14
  108.2 0.4 copy-done.1
  108.7 0.0 copy-start
  108.7 0.8 copy.15
  109.5 0.4 copy-done
  109.9 0.8 copy.16
Async XLA Ops:
  105.7 1.7 %copy-start.2 = (f32[1024,128]{1,0:T(8,128)S(1)}, f32[1024,128]{1,0:T(8,128)}, u32[]{:S(2)}) copy-start(f32[1024,128]{1,0:T(8,128)} %get-tuple-element.9) | copy-start | bytes 1572868
  107.4 1.2 %copy-start.1 = (f32[1024,128]{1,0:T(8,128)S(1)}, f32[1024,128]{1,0:T(8,128)}, u32[]{:S(2)}) copy-start(f32[1024,128]{1,0:T(8,128)} %get-tuple-element.10) | copy-start | bytes 1572868
  108.7 1.2 %copy-start = (f32[128,1024]{1,0:T(8,128)S(1)}, f32[128,1024]{1,0:T(8,128)}, u32[]{:S(2)}) copy-start(f32[128,1024]{1,0:T(8,128)} %get-tuple-element.11) | copy-start | bytes 1572868

commit v4 on v3

--- a/solution.py
+++ b/solution.py
@@ -14,7 +14,8 @@
 MESH = pl.DeviceIdType.MESH
 BF = jnp.bfloat16
 F32 = jnp.float32
-NSEM = 192
+NSEM = 224
+ZF = 64
 HOME = 128
 ROUNDS = ((0, 0, HOME, 256 - HOME), (0, 1, HOME, 256 - HOME), (1, 1, 0, 256), (1, 0, 0, 256))
 
@@ -24,7 +25,7 @@
 
 
 def kernel(factor, tok, og, wg, wu, wd, ig_o, gg_o, ug_o, dg_o,
-           own, xb, wgu, wdn, pgu, ph, pgur, phr, agu, ah, igp, sibr, farr, nearr, fs, zr, igs, igr,
+           own, xb, wgu, wdn, pgu, ph, pgur, phr, agu, ah, igp, sibr, farr, nearr, fs, zfr, zr, igs, igr,
            ws, hs, gb, hb, gfr, hfr, gnr, hnr, lsem, ssem, rsem):
     R, C = tok.shape
     F = wg.shape[1]
@@ -150,7 +151,7 @@
     def ysend(w):
         for h in range(2):
             send(("y", w, 0, h), wchunk(w, y, h), wchunk(w, y, h), d_yr)
-            send(("y", w, 1, h), wchunk(w, y, h), wchunk(w, y, h), d_yl)
+            send(("y", w, 1, 1 - h), wchunk(w, y, 1 - h), wchunk(w, y, 1 - h), d_yl)
 
     def yfwd(w):
         recv(("y", w, 0, 0), wchunk(w, yl, 0))
@@ -167,7 +168,7 @@
     def hsend():
         for h in range(2):
             send(("h", 0, h), home(x, h), home(x, h), d_xr)
-            send(("h", 1, h), home(x, h), home(x, h), d_xl)
+            send(("h", 1, 1 - h), home(x, 1 - h), home(x, 1 - h), d_xl)
 
     def homez(j, xp):
         send(("hz", j), home(xp), xb.at[0, 2 * xp + core, rows(z_hi * R, HOME), :], d_zs, rs=8 + 4 * inner + j)
@@ -190,30 +191,41 @@
 
     xorder = (x, xl, xr, xf)
 
-    def hz(rel):
-        t = t_of[rel]
-        for j, xp in enumerate(xorder):
-            p = part(0, xp, core, t, 0, HOME)
-            if rel == 0:
-                @pl.when(is_inner)
-                def _():
-                    recv(("zh", j), p)
-            else:
-                recv(("zh", 4 + j), p)
-
-                @pl.when(is_inner)
-                def _():
-                    send(("hzr", j), p, p, d_zlo, rs=12 + j, wait_later=False)
-            send(("hs", rel, j), p, p, d_sib)
+    def hpart(rel, j):
+        return part(0, xorder[j], core, t_of[rel], 0, HOME)
+
+    def hsib(rel, j):
+        send(("hs", rel, j), hpart(rel, j), hpart(rel, j), d_sib, wait_later=False)
+
+    def hz_inner(j):
+        @pl.when(is_inner)
+        def _():
+            recv(("zh", 4 + j), hpart(1, j))
+            send(("hzr", j), hpart(1, j), hpart(1, j), d_zlo, rs=12 + j, wait_later=False)
+            hsib(1, j)
+            recv(("zh", j), hpart(0, j))
+            hsib(0, j)
+
+    def hz_outer(j):
+        @pl.when(is_outer)
+        def _():
+            recv(("zh", 4 + j), hpart(1, j))
+            hsib(1, j)
+
+    def hs_outer():
+        @pl.when(is_outer)
+        def _():
+            for j in range(4):
+                hsib(0, j)
 
     def hsfin(rel):
         for j, xp in enumerate(xorder):
             recv(("hs", rel, j), part(0, xp, oc, t_of[rel], 0, HOME))
 
-    def relay(r):
+    def relay(r, hs=(0, 1)):
         a, rel, r0, n = ROUNDS[r]
         t = t_of[rel]
-        for h in range(2):
+        for h in hs:
             k = 2 * a + h
 
             @pl.when(is_inner)
@@ -236,8 +248,13 @@
                 @pl.when(is_outer)
                 def _():
                     recv(("z", 4 + k), c)
-            send(("x", r, 0, h), c, c, d_xr)
-            send(("x", r, 1, h), c, c, d_xl)
+            if h == 0:
+                send(("x", r, 0, 0), c, c, d_xr)
+            else:
+                send(("x", r, 1, 1), c, c, d_xl)
+                send(("x", r, 0, 1), c, c, d_xr)
+                c = chunk(a, x, t, 0, r0, n)
+                send(("x", r, 1, 0), c, c, d_xl)
         p = part(a, x, core, t, r0, n)
         send(("s", r, 0), p, p, d_sib)
 
@@ -296,30 +313,36 @@
     relay(1)
     xsend(1)
     hfin()
-    relay(2)
+    hs_outer()
+    relay(2, (0,))
     yfwd(0)
     ysend(1)
     xfwd(0)
+    relay(2, (1,))
     xsend(2)
-    xfin(0)
+    hz_inner(0)
     xfwd(1)
     xsend(3)
+    xfin(0)
+    hz_inner(1)
     xfin(1)
+    hz_inner(2)
     xfwd(2)
-    hz(0)
-    hz(1)
+    hz_inner(3)
     yfwd(1)
+    xfwd(3)
     yfin(0)
     sfin(0)
     sfin(1)
-    xfin(2)
-    xfwd(3)
+    for j in range(4):
+        hz_outer(j)
     hsfin(0)
     hsfin(1)
     forward(1)
     send("pgu", pgu.at[1], pgur, d_zhi)
     forward(0)
     yfin(1)
+    xfin(2)
     sfin(2)
     forward(2)
     send("ph", ph.at[1], phr, d_zhi)
@@ -342,53 +365,78 @@
     send("ah", ah.at[trow(z_hi), :], ah.at[trow(z_hi), :], d_zhi)
 
     order = (xf, xr, xl, x)
+    RA = ((ZF, R - ZF), (0, ZF))
+
+    def hrows(p, h):
+        r0, n = RA[p]
+        return pl.ds(r0 + h * (n // 2), n // 2)
+
+    def arows(p):
+        return pl.ds(*RA[p])
+
+    def igblock(rel, xp, c):
+        w = wgu[xp, pl.ds(pl.multiple_of(c * C, C), C), :]
+        igp[rel, 2 * xp + c] = dot(agu[trow(t_of[rel]), :], w, 1, 1)
 
     def igstart(rel):
-        def step(e, carry):
-            igp[rel, e] = dot(agu[trow(t_of[rel]), :], wgu[e // 2, half(e), :], 1, 1)
-            return carry
-
-        lax.fori_loop(0, 2 * nx, step, 0)
         for j, xp in enumerate(order):
+            igblock(rel, xp, oc)
             send(("is", rel, j), igp.at[rel, 2 * xp + oc], sibr.at[rel, xp], d_sib)
+        for xp in order:
+            igblock(rel, xp, core)
 
     def addsib(rel, j):
         xp = order[j]
         recv(("is", rel, j), sibr.at[rel, xp])
         igp[rel, 2 * xp + core] += sibr[rel, xp]
 
-    def hrow(h):
-        return pl.ds(h * H, H)
-
-    def igfirst(rel):
+    def zfirst(rel, j):
+        xp = order[j]
+        send(("zf", j), igp.at[rel, 2 * xp + core, arows(1), :], zfr.at[xp], d_zlo, wait_later=False)
+
+    def igfar(p, rel, k):
+        for h, d in enumerate((d_xr, d_xl)):
+            fs[k, h, pl.ds(0, RA[p][1] // 2), :] = igp[rel, 2 * xf + core, hrows(p, h), :].astype(BF)
+            n = pl.ds(0, RA[p][1] // 2)
+            send(("if", k, h), fs.at[k, h, n, :], farr.at[k, h, n, :], d)
+
+    def ignear(p, rel, k):
+        for h, (xp, d) in enumerate(((xr, d_xr), (xl, d_xl))):
+            send(("in", k, h, 1 - h), igp.at[rel, 2 * xp + core, hrows(p, 1 - h), :],
+                 nearr.at[rel, h, hrows(p, 1 - h), :], d)
+
+    def igsecond(p, rel, k):
+        for h, (xp, d) in enumerate(((xr, d_xr), (xl, d_xl))):
+            n = pl.ds(0, RA[p][1] // 2)
+            recv(("if", k, h), farr.at[k, h, n, :])
+            igp[rel, 2 * xp + core, hrows(p, h), :] += farr[k, h, n, :].astype(F32)
+            send(("in", k, h, h), igp.at[rel, 2 * xp + core, hrows(p, h), :], nearr.at[rel, h, hrows(p, h), :], d)
+
+    def iglast(p, rel, k):
+        for h in range(2):
+            for g in range(2):
+                recv(("in", k, h, g), nearr.at[rel, h, hrows(p, g), :])
+        igp[rel, 2 * x + core, arows(p), :] += nearr[rel, 0, arows(p), :] + nearr[rel, 1, arows(p), :]
+
+    def igfirst(rel, when):
         addsib(rel, 0)
-        for h, d in enumerate((d_xr, d_xl)):
-            fs[rel, h] = igp[rel, 2 * xf + core, hrow(h), :].astype(BF)
-            send(("if", rel, h), fs.at[rel, h], farr.at[rel, h], d)
-        for h, (j, xp, d) in enumerate(((1, xr, d_xr), (2, xl, d_xl))):
-            addsib(rel, j)
-            send(("in", rel, h, 1 - h), igp.at[rel, 2 * xp + core, hrow(1 - h), :],
-                 nearr.at[rel, h, hrow(1 - h), :], d)
-
-    def igsecond(rel):
-        for h, (xp, d) in enumerate(((xr, d_xr), (xl, d_xl))):
-            recv(("if", rel, h), farr.at[rel, h])
-            igp[rel, 2 * xp + core, hrow(h), :] += farr[rel, h].astype(F32)
-            send(("in", rel, h, h), igp.at[rel, 2 * xp + core, hrow(h), :], nearr.at[rel, h, hrow(h), :], d)
+        igfar(0, rel, rel)
+        addsib(rel, 1)
+        addsib(rel, 2)
+        ignear(0, rel, rel)
         addsib(rel, 3)
 
-    def iglast(rel):
-        for h in range(2):
-            for g in range(2):
-                recv(("in", rel, h, g), nearr.at[rel, h, hrow(g), :])
-        igp[rel, 2 * x + core] += nearr[rel, 0] + nearr[rel, 1]
+        @pl.when(when)
+        def _():
+            for j in range(4):
+                zfirst(rel, j)
 
     igstart(0)
-    igfirst(0)
+    igfirst(0, is_inner)
     recv("agu", agu.at[trow(1 - z_hi), :])
     recv("ah", ah.at[trow(1 - z_hi), :])
     igstart(1)
-    igfirst(1)
+    igfirst(1, is_outer)
 
     def wstep(e, carry):
         g = dot(xb[0, e, : 2 * R], agu[...], 0, 0)
@@ -408,8 +456,16 @@
         send(("gn", h, 1 - h), gb.at[2 * yp + 1 - h], gnr.at[h, 1 - h], d)
         send(("hn", h, 1 - h), hb.at[2 * yp + 1 - h], hnr.at[h, 1 - h], d)
 
-    igsecond(1)
-    igsecond(0)
+    igsecond(0, 1, 1)
+    igsecond(0, 0, 0)
+    keep = inner
+    for j in (0, 1, 2, 3):
+        xp = order[j]
+        recv(("zf", j), zfr.at[xp])
+        igp[keep, 2 * xp + core, arows(1), :] += zfr[xp]
+        if j == 0:
+            igfar(1, keep, 2)
+    ignear(1, keep, 2)
 
     for h, (yp, d) in enumerate(sides):
         recv(("gf", h), gfr.at[h])
@@ -421,27 +477,37 @@
 
     def zsend(rel):
         for h in range(2):
-            send(("zi", rel, h), igp.at[rel, 2 * x + core, hrow(h), :], zr.at[hrow(h), :], d_zlo,
+            send(("zi", rel, h), igp.at[rel, 2 * x + core, hrows(0, h), :], zr.at[hrows(0, h), :], d_zlo,
                  rs=sid(("zir", h)), wait_later=False)
 
-    iglast(1)
+    iglast(0, 1, 1)
 
     @pl.when(is_outer)
     def _():
         zsend(1)
 
-    iglast(0)
+    igsecond(1, keep, 2)
+    iglast(0, 0, 0)
 
     @pl.when(is_inner)
     def _():
         zsend(0)
 
+    iglast(1, keep, 2)
+
     @pl.when(is_inner)
     def _():
-        for h in range(2):
-            recv(("zir", h), zr.at[hrow(h), :])
-            igs[hrow(h), :] = (igp[1, 2 * x + core, hrow(h), :] + zr[hrow(h), :]).astype(BF)
-            send(("zo", h), igs.at[hrow(h), :], igr.at[hrow(h), :], d_zz, wait_later=False)
+        igs[2, pl.ds(0, ZF), :] = igp[1, 2 * x + core, arows(1), :].astype(BF)
+        send(("zo", 2), igs.at[2, pl.ds(0, ZF), :], igr.at[2, pl.ds(0, ZF), :], d_zz, wait_later=False)
+        n = pl.ds(0, (R - ZF) // 2)
+        for h in range(2):
+            recv(("zir", h), zr.at[hrows(0, h), :])
+            igs[h, n, :] = (igp[1, 2 * x + core, hrows(0, h), :] + zr[hrows(0, h), :]).astype(BF)
+            send(("zo", h), igs.at[h, n, :], igr.at[h, n, :], d_zz, wait_later=False)
+
+    @pl.when(is_outer)
+    def _():
+        ig_o[arows(1), :] = igp[0, 2 * x + core, arows(1), :].astype(BF)
 
     for h in range(2):
         for s in range(2):
@@ -455,8 +521,8 @@
     @pl.when(is_outer)
     def _():
         for h in range(2):
-            recv(("zir", h), zr.at[hrow(h), :])
-            ig_o[hrow(h), :] = (igp[0, 2 * x + core, hrow(h), :] + zr[hrow(h), :]).astype(BF)
+            recv(("zir", h), zr.at[hrows(0, h), :])
+            ig_o[hrows(0, h), :] = (igp[0, 2 * x + core, hrows(0, h), :] + zr[hrows(0, h), :]).astype(BF)
 
     def wait_send(name, src):
         i = sid(name)
@@ -466,24 +532,32 @@
 
     @pl.when(is_inner)
     def _():
-        for h in range(2):
-            recv(("zo", h), igr.at[hrow(h), :])
-        ig_o[...] = igr[...]
-        for h in range(2):
-            wait_send(("zo", h), igs.at[hrow(h), :])
-            wait_send(("zi", 0, h), zr.at[hrow(h), :])
+        zs, n = pl.ds(0, ZF), pl.ds(0, (R - ZF) // 2)
+        recv(("zo", 2), igr.at[2, zs, :])
+        ig_o[arows(1), :] = igr[2, zs, :]
+        for h in range(2):
+            recv(("zo", h), igr.at[h, n, :])
+            ig_o[hrows(0, h), :] = igr[h, n, :]
+        wait_send(("zo", 2), igs.at[2, zs, :])
+        for h in range(2):
+            wait_send(("zo", h), igs.at[h, n, :])
+            wait_send(("zi", 0, h), zr.at[hrows(0, h), :])
         for r in (1, 2):
             a, rel, r0, n = ROUNDS[r]
             for h in range(2):
                 wait_send(("zr", 2 * a + h), chunk(a, x, t_of[1], h, r0, n))
-        for j, xp in enumerate(xorder):
-            wait_send(("hzr", j), part(0, xp, core, t_of[1], 0, HOME))
+        for j in range(4):
+            wait_send(("hzr", j), hpart(1, j))
 
     @pl.when(is_outer)
     def _():
         for h in range(2):
-            wait_send(("zi", 1, h), zr.at[hrow(h), :])
-
+            wait_send(("zi", 1, h), zr.at[hrows(0, h), :])
+
+    for j in range(4):
+        wait_send(("zf", j), zfr.at[j])
+        for rel in range(2):
+            wait_send(("hs", rel, j), hpart(rel, j))
     for c in pending:
         c.wait_send()
     assert len(ids) <= NSEM
@@ -501,8 +575,8 @@
         V((2, R, C), BF), V((2, 8, 2 * R + HOME, C), BF), V((4, 2 * C, 2 * F), BF), V((4, F, 2 * C), BF),
         V((2, R, 2 * F), F32), V((2, R, F), F32), V((R, 2 * F), F32), V((R, F), F32),
         V((2 * R, 2 * F), BF), V((2 * R, F), BF),
-        V((2, 8, R, C), F32), V((2, 4, R, C), F32), V((2, 2, H, C), BF), V((2, 2, R, C), F32), V((2, 2, H, C), BF),
-        V((R, C), F32), V((R, C), BF), V((R, C), BF),
+        V((2, 8, R, C), F32), V((2, 4, R, C), F32), V((3, 2, H, C), BF), V((2, 2, R, C), F32), V((3, 2, H, C), BF), V((4, ZF, C), F32),
+        V((R, C), F32), V((3, H, C), BF), V((3, H, C), BF),
         V((8, C, 2 * F), F32), V((8, F, C), F32), V((8, C, 2 * F), BF), V((8, F, C), BF),
         V((2, C, 2 * F), BF), V((2, F, C), BF), V((2, 2, C, 2 * F), BF), V((2, 2, F, C), BF),
         pltpu.SemaphoreType.DMA((8,)), pltpu.SemaphoreType.DMA((NSEM,)), pltpu.SemaphoreType.DMA((NSEM,)),

time: 111 us -> 103 us (0.928)
  Pallas kernels: 105 us -> 96.1 us
    pallas_call x1, Pallas kernels: 105 us -> 96.1 us  [shards(): pl.pallas_call(functools.partial(kernel, factor), out_shape=(jax.ShapeDty...]
where the time goes in v4:
time: 103 us; the launch traced here: 102 us
  Pallas kernels  96.1 us (93%)
  local copies, waits for them, and re-layouts  4.98 us (5%)
    pallas_call x1, Pallas kernels, shards(): pl.pallas_call(functools.partial(kernel, factor), out_shape=(jax.ShapeDty...  96.1 us
    unnamed x10, local copies, waits for them, and re-layouts  4.98 us

profile of v4, /device:TPU:1, one launch (start us, length us, event | category | flops | bytes accessed | tf_op | source)
XLA Modules:
  0.0 101.8 jit_solution(10102421478751492625)
XLA Ops:
  0.6 96.1 %ffn_backward.1 = (bf16[256,512]{1,0:T(8,128)(2,1)}, f32[1024,128]{1,0:T(8,128)}, f32[1024,128]{1,0:T(8,128)}, f32[128,1024]{1,0:T(8,128)}) custom-call(bf16[256,512]{1,0:T(8,128)(2,1)} %tok.1, bf16[256,512]{1,0:T(8,128)(2,1)} %og.1, bf16[1024,128]{1,0:T(8,128)(2,1)} %wg.1, bf16[1024,128]{1,0:T(8,128)(2,1)} %wu.1, bf16[128,1024]{1,0:T(8,128)(2,1)} %wd.1), custom_call_target="tpu_custom_call" | custom-call | tf_op jit(solution)/shard_map/ffn_backward/pallas_call | solution.py:584
  96.8 0.0 copy-start.2
  96.8 1.7 %copy.13 = bf16[256,512]{1,0:T(8,128)(2,1)} copy(bf16[256,512]{1,0:T(8,128)(2,1)} %get-tuple-element.8) | data formatting | bytes 524288
  98.5 0.0 copy-done.2
  98.5 0.0 copy-start.1
  98.5 0.8 copy.14
  99.3 0.4 copy-done.1
  99.8 0.0 copy-start
  99.8 0.8 copy.15
  100.6 0.4 copy-done
  101.0 0.8 copy.16
Async XLA Ops:
  96.8 1.7 %copy-start.2 = (f32[1024,128]{1,0:T(8,128)S(1)}, f32[1024,128]{1,0:T(8,128)}, u32[]{:S(2)}) copy-start(f32[1024,128]{1,0:T(8,128)} %get-tuple-element.9) | copy-start | bytes 1572868
  98.5 1.2 %copy-start.1 = (f32[1024,128]{1,0:T(8,128)S(1)}, f32[1024,128]{1,0:T(8,128)}, u32[]{:S(2)}) copy-start(f32[1024,128]{1,0:T(8,128)} %get-tuple-element.10) | copy-start | bytes 1572868
  99.8 1.2 %copy-start = (f32[128,1024]{1,0:T(8,128)S(1)}, f32[128,1024]{1,0:T(8,128)}, u32[]{:S(2)}) copy-start(f32[128,1024]{1,0:T(8,128)} %get-tuple-element.11) | copy-start | bytes 1572868

commit v5 on v4

--- a/solution.py
+++ b/solution.py
@@ -16,8 +16,8 @@
 F32 = jnp.float32
 NSEM = 224
 ZF = 64
-HOME = 128
-ROUNDS = ((0, 0, HOME, 256 - HOME), (0, 1, HOME, 256 - HOME), (1, 1, 0, 256), (1, 0, 0, 256))
+HOME = 160
+ROUNDS = ((0, 0, 0, 256), (0, 1, 0, 256), (1, 0, HOME, 256 - HOME), (1, 1, HOME, 256 - HOME))
 
 
 def dot(a, b, ca, cb):
@@ -93,8 +93,8 @@
 
     def home(xp, h=None):
         if h is None:
-            return xb.at[0, 2 * xp + core, rows(home_at, HOME), :]
-        return xb.at[0, 2 * xp + core, rows(home_at + h * (HOME // 2), HOME // 2), :]
+            return xb.at[1, 2 * xp + core, rows(home_at, HOME), :]
+        return xb.at[1, 2 * xp + core, rows(home_at + h * (HOME // 2), HOME // 2), :]
 
     loads_w = [
         pltpu.make_async_copy(wg, wgu.at[y, :, pl.ds(0, F)], lsem.at[0]),
@@ -109,10 +109,10 @@
         c.start()
 
     outer_loads = (
-        (tok.at[pl.ds(HOME, R - HOME), :], part(0, x, core, z_hi, HOME, R - HOME), lsem.at[5]),
-        (og, blk(1, x, core, z_hi), lsem.at[6]),
+        (tok, blk(0, x, core, z_hi), lsem.at[5]),
+        (og.at[pl.ds(HOME, R - HOME), :], part(1, x, core, z_hi, HOME, R - HOME), lsem.at[6]),
     )
-    load_home = pltpu.make_async_copy(tok.at[pl.ds(0, HOME), :], home(x), lsem.at[7])
+    load_home = pltpu.make_async_copy(og.at[pl.ds(0, HOME), :], home(x), lsem.at[7])
     load_home.start()
 
     @pl.when(is_outer)
@@ -129,7 +129,7 @@
         c.wait()
     load_home.wait()
 
-    for a, rel, r0, n in (ROUNDS[0], ROUNDS[3]):
+    for a, rel, r0, n in (ROUNDS[0], ROUNDS[2]):
         for h in range(2):
             k = 2 * a + h
             send(("zs", k), own.at[a, pl.ds(r0 + h * (n // 2), n // 2), :], chunk(a, x, z_hi, h, r0, n), d_zs,
@@ -171,7 +171,7 @@
             send(("h", 1, 1 - h), home(x, 1 - h), home(x, 1 - h), d_xl)
 
     def homez(j, xp):
-        send(("hz", j), home(xp), xb.at[0, 2 * xp + core, rows(z_hi * R, HOME), :], d_zs, rs=8 + 4 * inner + j)
+        send(("hz", j), home(xp), xb.at[1, 2 * xp + core, rows(z_hi * R, HOME), :], d_zs, rs=8 + 4 * inner + j)
 
     def hfwd():
         recv(("h", 0, 0), home(xl, 0))
@@ -179,12 +179,14 @@
         recv(("h", 1, 1), home(xr, 1))
         send(("hf", 1), home(xr, 1), home(xr, 1), d_xl)
 
-    def hfin():
+    def hfin_a():
         homez(0, x)
         recv(("h", 0, 1), home(xl, 1))
         homez(1, xl)
         recv(("h", 1, 0), home(xr, 0))
         homez(2, xr)
+
+    def hfin_b():
         recv(("hf", 0), home(xf, 0))
         recv(("hf", 1), home(xf, 1))
         homez(3, xf)
@@ -192,7 +194,7 @@
     xorder = (x, xl, xr, xf)
 
     def hpart(rel, j):
-        return part(0, xorder[j], core, t_of[rel], 0, HOME)
+        return part(1, xorder[j], core, t_of[rel], 0, HOME)
 
     def hsib(rel, j):
         send(("hs", rel, j), hpart(rel, j), hpart(rel, j), d_sib, wait_later=False)
@@ -220,7 +222,7 @@
 
     def hsfin(rel):
         for j, xp in enumerate(xorder):
-            recv(("hs", rel, j), part(0, xp, oc, t_of[rel], 0, HOME))
+            recv(("hs", rel, j), part(1, xp, oc, t_of[rel], 0, HOME))
 
     def relay(r, hs=(0, 1)):
         a, rel, r0, n = ROUNDS[r]
@@ -234,29 +236,32 @@
                 recv(("z", 4 + k), c)
                 send(("zr", k), c, c, d_zlo, rs=4 + k, wait_later=False)
 
-    def xsend(r):
+    def xsend_h(r, h):
         a, rel, r0, n = ROUNDS[r]
         t = t_of[rel]
-        for h in range(2):
-            k = 2 * a + h
-            c = chunk(a, x, t, h, r0, n)
-            if rel == 0:
-                @pl.when(is_inner)
-                def _():
-                    recv(("z", k), c)
-            else:
-                @pl.when(is_outer)
-                def _():
-                    recv(("z", 4 + k), c)
-            if h == 0:
-                send(("x", r, 0, 0), c, c, d_xr)
-            else:
-                send(("x", r, 1, 1), c, c, d_xl)
-                send(("x", r, 0, 1), c, c, d_xr)
-                c = chunk(a, x, t, 0, r0, n)
-                send(("x", r, 1, 0), c, c, d_xl)
-        p = part(a, x, core, t, r0, n)
-        send(("s", r, 0), p, p, d_sib)
+        k = 2 * a + h
+        c = chunk(a, x, t, h, r0, n)
+        if rel == 0:
+            @pl.when(is_inner)
+            def _():
+                recv(("z", k), c)
+        else:
+            @pl.when(is_outer)
+            def _():
+                recv(("z", 4 + k), c)
+        if h == 0:
+            send(("x", r, 0, 0), c, c, d_xr)
+        else:
+            send(("x", r, 1, 1), c, c, d_xl)
+            send(("x", r, 0, 1), c, c, d_xr)
+            c = chunk(a, x, t, 0, r0, n)
+            send(("x", r, 1, 0), c, c, d_xl)
+            p = part(a, x, core, t, r0, n)
+            send(("s", r, 0), p, p, d_sib)
+
+    def xsend(r):
+        xsend_h(r, 0)
+        xsend_h(r, 1)
 
     def xfwd(r):
         a, rel, r0, n = ROUNDS[r]
@@ -287,82 +292,80 @@
         for j, xp in enumerate(xorder):
             recv(("s", r, j), part(a, xp, oc, t_of[rel], r0, n))
 
-    def half(e):
-        return pl.ds(pl.multiple_of(lax.rem(e, 2) * C, C), C)
-
-    def forward(r):
-        a, rel, r0, n = ROUNDS[r]
+    def forward(a, rel, r0, n):
         t = t_of[rel]
-        out = (pgu, ph)[a].at[rel]
-        out[...] = jnp.zeros(out.shape, F32)
-
-        def step(e, carry):
-            block = xb[a, e, trow(t), :]
+        terms = []
+        for e in range(2 * nx):
+            block = xb[a, e, rows(t * R + r0, n), :]
+            cols = pl.ds((e % 2) * C, C)
             if a == 0:
-                out[...] += dot(block, wgu[e // 2, half(e), :], 1, 0)
+                terms.append(dot(block, wgu[e // 2, cols, :], 1, 0))
             else:
-                out[...] += dot(block, wdn[e // 2, :, half(e)], 1, 1)
-            return carry
-
-        lax.fori_loop(0, 2 * nx, step, 0)
+                terms.append(dot(block, wdn[e // 2, :, cols], 1, 1))
+        (pgu, ph)[a][rel, pl.ds(r0, n)] = functools.reduce(jnp.add, terms)
+
+    REST = (HOME, R - HOME)
 
     hsend()
     ysend(0)
-    xsend(0)
+    xsend_h(0, 0)
+    relay(1, (0,))
     hfwd()
-    relay(1)
-    xsend(1)
-    hfin()
-    hs_outer()
-    relay(2, (0,))
+    xsend_h(0, 1)
+    relay(1, (1,))
+    hfin_a()
     yfwd(0)
     ysend(1)
+    relay(3)
     xfwd(0)
-    relay(2, (1,))
     xsend(2)
+    xsend(1)
+    xsend(3)
+    hfin_b()
+    hs_outer()
     hz_inner(0)
-    xfwd(1)
-    xsend(3)
+    hz_inner(1)
     xfin(0)
-    hz_inner(1)
-    xfin(1)
+    xfwd(2)
     hz_inner(2)
-    xfwd(2)
-    hz_inner(3)
-    yfwd(1)
-    xfwd(3)
     yfin(0)
     sfin(0)
-    sfin(1)
+    hz_inner(3)
+    forward(0, 0, 0, R)
+    send("pgu", pgu.at[0], pgur, d_zhi)
+    yfwd(1)
+    xfwd(1)
+    xfwd(3)
+    xfin(2)
+    sfin(2)
+    hsfin(0)
+    yfin(1)
+    forward(1, 0, 0, R)
+    send("ph", ph.at[0], phr, d_zhi)
+    xfin(1)
     for j in range(4):
         hz_outer(j)
-    hsfin(0)
+    xfin(3)
+    sfin(1)
+    forward(0, 1, 0, R)
     hsfin(1)
-    forward(1)
-    send("pgu", pgu.at[1], pgur, d_zhi)
-    forward(0)
-    yfin(1)
-    xfin(2)
-    sfin(2)
-    forward(2)
-    send("ph", ph.at[1], phr, d_zhi)
-    xfin(3)
+    forward(1, 1, 0, HOME)
     sfin(3)
-    forward(3)
+    forward(1, 1, *REST)
 
     recv("pgu", pgur)
     recv("ph", phr)
-    gate = pgu[0, :, :F] + pgur[:, :F]
-    up = pgu[0, :, F:] + pgur[:, F:]
-    hg = ph[0] + phr[...]
+    gate = pgu[1, :, :F] + pgur[:, :F]
+    up = pgu[1, :, F:] + pgur[:, F:]
+    hg = ph[1] + phr[...]
     squashed = jax.nn.sigmoid(gate)
     activated = gate * squashed
     slope = squashed * (1.0 + gate * (1.0 - squashed))
-    agu[trow(z_hi), :F] = (hg * up * slope).astype(BF)
-    agu[trow(z_hi), F:] = (hg * activated).astype(BF)
-    ah[trow(z_hi), :] = (activated * up).astype(BF)
-    send("agu", agu.at[trow(z_hi), :], agu.at[trow(z_hi), :], d_zhi)
-    send("ah", ah.at[trow(z_hi), :], ah.at[trow(z_hi), :], d_zhi)
+    agu[trow(1 - z_hi), :F] = (hg * up * slope).astype(BF)
+    agu[trow(1 - z_hi), F:] = (hg * activated).astype(BF)
+    ah[trow(1 - z_hi), :] = (activated * up).astype(BF)
+    send("agu", agu.at[trow(1 - z_hi), :], agu.at[trow(1 - z_hi), :], d_zhi)
+    send("ah", ah.at[trow(1 - z_hi), :], ah.at[trow(1 - z_hi), :], d_zhi)
 
     order = (xf, xr, xl, x)
     RA = ((ZF, R - ZF), (0, ZF))
@@ -431,79 +434,90 @@
             for j in range(4):
                 zfirst(rel, j)
 
-    igstart(0)
-    igfirst(0, is_inner)
-    recv("agu", agu.at[trow(1 - z_hi), :])
-    recv("ah", ah.at[trow(1 - z_hi), :])
-    igstart(1)
-    igfirst(1, is_outer)
-
-    def wstep(e, carry):
+    def wunit(e):
         g = dot(xb[0, e, : 2 * R], agu[...], 0, 0)
         ws[e] = g
         gb[e] = g.astype(BF)
         d = dot(ah[...], xb[1, e, : 2 * R], 0, 0)
         hs[e] = d
         hb[e] = d.astype(BF)
-        return carry
-
-    lax.fori_loop(0, 2 * ny, wstep, 0)
+
     sides = ((yr, d_yr), (yl, d_yl))
-    for h, (yp, d) in enumerate(sides):
-        send(("gf", h), gb.at[2 * yf + h], gfr.at[h], d)
-        send(("hf", h), hb.at[2 * yf + h], hfr.at[h], d)
-    for h, (yp, d) in enumerate(sides):
-        send(("gn", h, 1 - h), gb.at[2 * yp + 1 - h], gnr.at[h, 1 - h], d)
-        send(("hn", h, 1 - h), hb.at[2 * yp + 1 - h], hnr.at[h, 1 - h], d)
-
-    igsecond(0, 1, 1)
-    igsecond(0, 0, 0)
-    keep = inner
-    for j in (0, 1, 2, 3):
+    def zsend(rel):
+        for h in range(2):
+            send(("zi", rel, h), igp.at[rel, 2 * x + core, hrows(0, h), :], zr.at[hrows(0, h), :], d_zlo,
+                 rs=sid(("zir", h)), wait_later=False)
+
+    def wfirst(e, s, h):
+        wunit(e)
+        send(("gn", s, h), gb.at[e], gnr.at[s, h], sides[s][1])
+        send(("hn", s, h), hb.at[e], hnr.at[s, h], sides[s][1])
+
+    def zfadd(j):
         xp = order[j]
         recv(("zf", j), zfr.at[xp])
         igp[keep, 2 * xp + core, arows(1), :] += zfr[xp]
-        if j == 0:
-            igfar(1, keep, 2)
-    ignear(1, keep, 2)
-
-    for h, (yp, d) in enumerate(sides):
+
+    def wsecond(h):
+        yp, d = sides[h]
         recv(("gf", h), gfr.at[h])
         gb[2 * yp + h] = (ws[2 * yp + h] + gfr[h].astype(F32)).astype(BF)
         send(("gn", h, h), gb.at[2 * yp + h], gnr.at[h, h], d)
-        recv(("hf", h), hfr.at[h])
+        recv(("hf2", h), hfr.at[h])
         hb[2 * yp + h] = (hs[2 * yp + h] + hfr[h].astype(F32)).astype(BF)
         send(("hn", h, h), hb.at[2 * yp + h], hnr.at[h, h], d)
 
-    def zsend(rel):
-        for h in range(2):
-            send(("zi", rel, h), igp.at[rel, 2 * x + core, hrows(0, h), :], zr.at[hrows(0, h), :], d_zlo,
-                 rs=sid(("zir", h)), wait_later=False)
-
+    keep = inner
+    igstart(1)
+    igfirst(1, is_outer)
+    recv("agu", agu.at[trow(z_hi), :])
+    recv("ah", ah.at[trow(z_hi), :])
+    for h, (yp, d) in enumerate(sides):
+        wunit(2 * yf + h)
+        send(("gf", h), gb.at[2 * yf + h], gfr.at[h], d)
+        send(("hf2", h), hb.at[2 * yf + h], hfr.at[h], d)
+    igsecond(0, 1, 1)
+    igstart(0)
+    igfirst(0, is_inner)
+    for h, (yp, d) in enumerate(sides):
+        wfirst(2 * yp + 1 - h, h, 1 - h)
+    for h, (yp, d) in enumerate(sides):
+        wunit(2 * yp + h)
     iglast(0, 1, 1)
 
     @pl.when(is_outer)
     def _():
         zsend(1)
 
+    zfadd(0)
+    igfar(1, keep, 2)
+    wsecond(0)
+    wsecond(1)
+    igsecond(0, 0, 0)
+    zfadd(1)
+    zfadd(2)
+    ignear(1, keep, 2)
+    for h in range(2):
+        wunit(2 * y + h)
     igsecond(1, keep, 2)
     iglast(0, 0, 0)
 
     @pl.when(is_inner)
     def _():
         zsend(0)
-
-    iglast(1, keep, 2)
-
-    @pl.when(is_inner)
-    def _():
-        igs[2, pl.ds(0, ZF), :] = igp[1, 2 * x + core, arows(1), :].astype(BF)
-        send(("zo", 2), igs.at[2, pl.ds(0, ZF), :], igr.at[2, pl.ds(0, ZF), :], d_zz, wait_later=False)
         n = pl.ds(0, (R - ZF) // 2)
         for h in range(2):
             recv(("zir", h), zr.at[hrows(0, h), :])
             igs[h, n, :] = (igp[1, 2 * x + core, hrows(0, h), :] + zr[hrows(0, h), :]).astype(BF)
             send(("zo", h), igs.at[h, n, :], igr.at[h, n, :], d_zz, wait_later=False)
+
+    zfadd(3)
+    iglast(1, keep, 2)
+
+    @pl.when(is_inner)
+    def _():
+        igs[2, pl.ds(0, ZF), :] = igp[1, 2 * x + core, arows(1), :].astype(BF)
+        send(("zo", 2), igs.at[2, pl.ds(0, ZF), :], igr.at[2, pl.ds(0, ZF), :], d_zz, wait_later=False)
 
     @pl.when(is_outer)
     def _():
@@ -542,7 +556,7 @@
         for h in range(2):
             wait_send(("zo", h), igs.at[h, n, :])
             wait_send(("zi", 0, h), zr.at[hrows(0, h), :])
-        for r in (1, 2):
+        for r in (1, 3):
             a, rel, r0, n = ROUNDS[r]
             for h in range(2):
                 wait_send(("zr", 2 * a + h), chunk(a, x, t_of[1], h, r0, n))

time: 103 us -> 90 us (0.87)
  Pallas kernels: 96.1 us -> 83.9 us
    pallas_call x1, Pallas kernels: 96.1 us -> 83.9 us  [shards(): pl.pallas_call(functools.partial(kernel, factor), out_shape=(jax.ShapeDty...]
where the time goes in v5:
time: 90 us; the launch traced here: 89.5 us
  Pallas kernels  83.9 us (93%)
  local copies, waits for them, and re-layouts  4.98 us (6%)
    pallas_call x1, Pallas kernels, shards(): pl.pallas_call(functools.partial(kernel, factor), out_shape=(jax.ShapeDty...  83.9 us
    unnamed x10, local copies, waits for them, and re-layouts  4.98 us

profile of v5, /device:TPU:1, one launch (start us, length us, event | category | flops | bytes accessed | tf_op | source)
XLA Modules:
  0.0 89.5 jit_solution(3661463735263894467)
XLA Ops:
  0.6 83.9 %ffn_backward.1 = (bf16[256,512]{1,0:T(8,128)(2,1)}, f32[1024,128]{1,0:T(8,128)}, f32[1024,128]{1,0:T(8,128)}, f32[128,1024]{1,0:T(8,128)}) custom-call(bf16[256,512]{1,0:T(8,128)(2,1)} %tok.1, bf16[256,512]{1,0:T(8,128)(2,1)} %og.1, bf16[1024,128]{1,0:T(8,128)(2,1)} %wg.1, bf16[1024,128]{1,0:T(8,128)(2,1)} %wu.1, bf16[128,1024]{1,0:T(8,128)(2,1)} %wd.1), custom_call_target="tpu_custom_call" | custom-call | tf_op jit(solution)/shard_map/ffn_backward/pallas_call | solution.py:598
  84.5 0.0 copy-start.2
  84.5 1.7 %copy.13 = bf16[256,512]{1,0:T(8,128)(2,1)} copy(bf16[256,512]{1,0:T(8,128)(2,1)} %get-tuple-element.8) | data formatting | bytes 524288
  86.2 0.0 copy-done.2
  86.2 0.0 copy-start.1
  86.2 0.8 copy.14
  87.0 0.4 copy-done.1
  87.5 0.0 copy-start
  87.5 0.8 copy.15
  88.3 0.4 copy-done
  88.7 0.8 copy.16
Async XLA Ops:
  84.5 1.7 %copy-start.2 = (f32[1024,128]{1,0:T(8,128)S(1)}, f32[1024,128]{1,0:T(8,128)}, u32[]{:S(2)}) copy-start(f32[1024,128]{1,0:T(8,128)} %get-tuple-element.9) | copy-start | bytes 1572868
  86.2 1.2 %copy-start.1 = (f32[1024,128]{1,0:T(8,128)S(1)}, f32[1024,128]{1,0:T(8,128)}, u32[]{:S(2)}) copy-start(f32[1024,128]{1,0:T(8,128)} %get-tuple-element.10) | copy-start | bytes 1572868
  87.5 1.2 %copy-start = (f32[128,1024]{1,0:T(8,128)S(1)}, f32[128,1024]{1,0:T(8,128)}, u32[]{:S(2)}) copy-start(f32[128,1024]{1,0:T(8,128)} %get-tuple-element.11) | copy-start | bytes 1572868

commit v6 on v5

--- a/solution.py
+++ b/solution.py
@@ -577,6 +577,15 @@
     assert len(ids) <= NSEM
 
 
+def deliver(*refs):
+    n = (len(refs) - 1) // 2
+    copies = [pltpu.make_async_copy(refs[k], refs[n + k], refs[-1].at[k]) for k in range(n)]
+    for c in copies:
+        c.start()
+    for c in copies:
+        c.wait()
+
+
 def shards(tokens, out_grad, gate_weight, up_weight, down_weight):
     R, C = tokens.shape
     F = gate_weight.shape[1]
@@ -595,13 +604,13 @@
         V((2, C, 2 * F), BF), V((2, F, C), BF), V((2, 2, C, 2 * F), BF), V((2, 2, F, C), BF),
         pltpu.SemaphoreType.DMA((8,)), pltpu.SemaphoreType.DMA((NSEM,)), pltpu.SemaphoreType.DMA((NSEM,)),
     ]
-    return pl.pallas_call(
+    held = pl.pallas_call(
         functools.partial(kernel, factor),
         out_shape=(
-            jax.ShapeDtypeStruct((R, C), BF),
-            jax.ShapeDtypeStruct((2 * C, F), F32),
-            jax.ShapeDtypeStruct((2 * C, F), F32),
-            jax.ShapeDtypeStruct((F, 2 * C), F32),
+            V((R, C), BF),
+            V((2 * C, F), F32),
+            V((2 * C, F), F32),
+            V((F, 2 * C), F32),
         ),
         in_specs=[anyspec] * 5,
         out_specs=(vm,) * 4,
@@ -610,6 +619,14 @@
             collective_id=0, has_side_effects=True, vmem_limit_bytes=60 * 1024 * 1024),
         name="ffn_backward",
     )(tokens, out_grad, gate_weight, up_weight, down_weight)
+    return pl.pallas_call(
+        deliver,
+        out_shape=tuple(jax.ShapeDtypeStruct(a.shape, a.dtype) for a in held),
+        in_specs=[vm] * len(held),
+        out_specs=(anyspec,) * len(held),
+        scratch_shapes=[pltpu.SemaphoreType.DMA((len(held),))],
+        name="deliver",
+    )(*[pltpu.with_memory_space_constraint(a, pltpu.VMEM) for a in held])
 
 
 def solution(mesh):

time: 90 us -> 84.8 us (0.942)
  local copies, waits for them, and re-layouts: 4.98 us -> 0 us
    unnamed x10 -> x0, local copies, waits for them, and re-layouts: 4.98 us -> none
    pallas_call x1 -> x2, Pallas kernels: 83.9 us -> 83.9 us  [the longest x1 82.6 us: shards(): pl.pallas_call(functools.partial(kernel, factor), out_shape=(V((R, C), BF...]
where the time goes in v6:
time: 84.8 us; the launch traced here: 84.5 us
  Pallas kernels  83.9 us (99%)
    pallas_call x1, Pallas kernels, shards(): pl.pallas_call(functools.partial(kernel, factor), out_shape=(V((R, C), BF...  82.6 us

profile of v6, /device:TPU:1, one launch (start us, length us, event | category | flops | bytes accessed | tf_op | source)
XLA Modules:
  0.0 84.5 jit_solution(8114753834194132692)
XLA Ops:
  0.6 82.6 %ffn_backward.1 = (bf16[256,512]{1,0:T(8,128)(2,1)S(1)}, f32[1024,128]{1,0:T(8,128)S(1)}, f32[1024,128]{1,0:T(8,128)S(1)}, f32[128,1024]{1,0:T(8,128)S(1)}) custom-call(bf16[256,512]{1,0:T(8,128)(2,1)} %tok.1, bf16[256,512]{1,0:T(8,128)(2,1)} %og.1, bf16[1024,128]{1,0:T(8,128)(2,1)} %wg.1, bf16[1024,128]{1,0:T(8,128)(2,1)} %wu.1, bf16[128,1024]{1,0:T(8,128)(2,1)} %wd.1), custom_call_target="tpu_custom_call" | custom-call | tf_op jit(solution)/shard_map/ffn_backward/pallas_call | solution.py:607
  83.3 1.3 %deliver.1 = (bf16[256,512]{1,0:T(8,128)(2,1)}, f32[1024,128]{1,0:T(8,128)}, f32[1024,128]{1,0:T(8,128)}, f32[128,1024]{1,0:T(8,128)}) custom-call(bf16[256,512]{1,0:T(8,128)(2,1)S(1)} %get-tuple-element.8.refs_0_, f32[1024,128]{1,0:T(8,128)S(1)} %get-tuple-element.9.refs_1_, f32[1024,128]{1,0:T(8,128)S(1)} %get-tuple-element.10.refs_2_, ...), custom_call_target="tpu_custom_call" | custom-call | tf_op jit(solution)/shard_map/deliver/pallas_call | solution.py:622

commit v7 on v6

--- a/solution.py
+++ b/solution.py
@@ -14,7 +14,8 @@
 MESH = pl.DeviceIdType.MESH
 BF = jnp.bfloat16
 F32 = jnp.float32
-NSEM = 224
+NSEND, NRECV = 48, 96
+GROUP = 6
 ZF = 64
 HOME = 160
 ROUNDS = ((0, 0, 0, 256), (0, 1, 0, 256), (1, 0, HOME, 256 - HOME), (1, 1, HOME, 256 - HOME))
@@ -47,32 +48,57 @@
     d_zs = (z_lo, y, 1 - z_lo, x, core)
     partners = (d_xr, d_xl, d_yr, d_yl, d_sib, d_zlo, d_zhi, d_zz)
 
-    ids = {}
-
-    def sid(name):
-        return ids.setdefault(name, len(ids))
+    sends, recvs = {}, {}
+
+    def slot(table, name):
+        return table.setdefault(name, len(table))
 
     for k in range(8):
-        sid(("z", k))
+        slot(recvs, ("z", k))
     for k in range(8):
-        sid(("zh", k))
-    pending = []
+        slot(recvs, ("zh", k))
+    groups = []
+
+    def size(ref):
+        return math.prod(ref.shape) * jnp.dtype(ref.dtype).itemsize
+
+    def unit_of(nbytes):
+        k = nbytes // 16384
+        if nbytes % 16384 == 0:
+            for n in (8, 7, 6, 5, 4, 3, 2, 1):
+                if k % n == 0 and k // n <= 2 * R // 16:
+                    return n, 16 * (k // n)
+        return None
+
+    def wait_bytes(sem, nbytes):
+        n, m = unit_of(nbytes)
+        r = xb.at[0, pl.ds(0, n), pl.ds(0, m), :]
+        pltpu.make_async_copy(r, r, sem).wait()
+
+    def remote(src, dst, dev, i, j):
+        return pltpu.make_async_remote_copy(
+            src_ref=src, dst_ref=dst, send_sem=ssem.at[i], recv_sem=rsem.at[j],
+            device_id=dev, device_id_type=MESH)
 
     def send(name, src, dst, dev, rs=None, wait_later=True):
-        i = sid(name)
-        c = pltpu.make_async_remote_copy(
-            src_ref=src, dst_ref=dst, send_sem=ssem.at[i], recv_sem=rsem.at[i if rs is None else rs],
-            device_id=dev, device_id_type=MESH)
-        c.start()
         if wait_later:
-            pending.append(c)
-        return c
-
-    def recv(name, dst):
-        i = sid(name)
-        pltpu.make_async_remote_copy(
-            src_ref=dst, dst_ref=dst, send_sem=ssem.at[i], recv_sem=rsem.at[i],
-            device_id=d_sib, device_id_type=MESH).wait_recv()
+            total = sum(groups[-1]) if groups else 0
+            if not groups or ((len(groups[-1]) >= GROUP or total >= 1 << 21) and unit_of(total) is not None):
+                groups.append([])
+            groups[-1].append(size(src))
+            i = slot(sends, ("group", len(groups) - 1))
+        else:
+            i = slot(sends, name)
+        remote(src, dst, dev, i, slot(recvs, name) if rs is None else rs).start()
+
+    def recv(name, *dsts):
+        if len(dsts) == 1:
+            remote(dsts[0], dsts[0], d_sib, 0, slot(recvs, name)).wait_recv()
+        else:
+            wait_bytes(rsem.at[slot(recvs, name)], sum(size(d) for d in dsts))
+
+    def wait_send(name, src):
+        remote(src, src, d_sib, slot(sends, name), 0).wait_send()
 
     def trow(t):
         return pl.ds(pl.multiple_of(t * R, R), R)
@@ -150,20 +176,17 @@
 
     def ysend(w):
         for h in range(2):
-            send(("y", w, 0, h), wchunk(w, y, h), wchunk(w, y, h), d_yr)
-            send(("y", w, 1, 1 - h), wchunk(w, y, 1 - h), wchunk(w, y, 1 - h), d_yl)
+            send(("yf", w) if h else ("y", w, 0), wchunk(w, y, h), wchunk(w, y, h), d_yr)
+            send(("yf", w) if h else ("y", w, 1), wchunk(w, y, 1 - h), wchunk(w, y, 1 - h), d_yl)
 
     def yfwd(w):
-        recv(("y", w, 0, 0), wchunk(w, yl, 0))
-        send(("yf", w, 0), wchunk(w, yl, 0), wchunk(w, yl, 0), d_yr)
-        recv(("y", w, 1, 1), wchunk(w, yr, 1))
-        send(("yf", w, 1), wchunk(w, yr, 1), wchunk(w, yr, 1), d_yl)
+        recv(("y", w, 0), wchunk(w, yl, 0))
+        send(("yf", w), wchunk(w, yl, 0), wchunk(w, yl, 0), d_yr)
+        recv(("y", w, 1), wchunk(w, yr, 1))
+        send(("yf", w), wchunk(w, yr, 1), wchunk(w, yr, 1), d_yl)
 
     def yfin(w):
-        recv(("y", w, 0, 1), wchunk(w, yl, 1))
-        recv(("y", w, 1, 0), wchunk(w, yr, 0))
-        recv(("yf", w, 0), wchunk(w, yf, 0))
-        recv(("yf", w, 1), wchunk(w, yf, 1))
+        recv(("yf", w), wchunk(w, yl, 1), wchunk(w, yr, 0), wchunk(w, yf, 0), wchunk(w, yf, 1))
 
     def hsend():
         for h in range(2):
@@ -175,9 +198,9 @@
 
     def hfwd():
         recv(("h", 0, 0), home(xl, 0))
-        send(("hf", 0), home(xl, 0), home(xl, 0), d_xr)
+        send("hf", home(xl, 0), home(xl, 0), d_xr)
         recv(("h", 1, 1), home(xr, 1))
-        send(("hf", 1), home(xr, 1), home(xr, 1), d_xl)
+        send("hf", home(xr, 1), home(xr, 1), d_xl)
 
     def hfin_a():
         homez(0, x)
@@ -187,8 +210,7 @@
         homez(2, xr)
 
     def hfin_b():
-        recv(("hf", 0), home(xf, 0))
-        recv(("hf", 1), home(xf, 1))
+        recv("hf", home(xf, 0), home(xf, 1))
         homez(3, xf)
 
     xorder = (x, xl, xr, xf)
@@ -197,7 +219,7 @@
         return part(1, xorder[j], core, t_of[rel], 0, HOME)
 
     def hsib(rel, j):
-        send(("hs", rel, j), hpart(rel, j), hpart(rel, j), d_sib, wait_later=False)
+        send(("hs", rel, j), hpart(rel, j), hpart(rel, j), d_sib, rs=slot(recvs, ("hs", rel)), wait_later=False)
 
     def hz_inner(j):
         @pl.when(is_inner)
@@ -221,8 +243,7 @@
                 hsib(0, j)
 
     def hsfin(rel):
-        for j, xp in enumerate(xorder):
-            recv(("hs", rel, j), part(1, xp, oc, t_of[rel], 0, HOME))
+        recv(("hs", rel), *[part(1, xp, oc, t_of[rel], 0, HOME) for xp in xorder])
 
     def relay(r, hs=(0, 1)):
         a, rel, r0, n = ROUNDS[r]
@@ -257,7 +278,7 @@
             c = chunk(a, x, t, 0, r0, n)
             send(("x", r, 1, 0), c, c, d_xl)
             p = part(a, x, core, t, r0, n)
-            send(("s", r, 0), p, p, d_sib)
+            send(("s", r), p, p, d_sib)
 
     def xsend(r):
         xsend_h(r, 0)
@@ -268,29 +289,27 @@
         t = t_of[rel]
         c = chunk(a, xl, t, 0, r0, n)
         recv(("x", r, 0, 0), c)
-        send(("xf", r, 0), c, c, d_xr)
+        send(("xf", r), c, c, d_xr)
         c = chunk(a, xr, t, 1, r0, n)
         recv(("x", r, 1, 1), c)
-        send(("xf", r, 1), c, c, d_xl)
+        send(("xf", r), c, c, d_xl)
 
     def xfin(r):
         a, rel, r0, n = ROUNDS[r]
         t = t_of[rel]
         recv(("x", r, 0, 1), chunk(a, xl, t, 1, r0, n))
         p = part(a, xl, core, t, r0, n)
-        send(("s", r, 1), p, p, d_sib)
+        send(("s", r), p, p, d_sib)
         recv(("x", r, 1, 0), chunk(a, xr, t, 0, r0, n))
         p = part(a, xr, core, t, r0, n)
-        send(("s", r, 2), p, p, d_sib)
-        recv(("xf", r, 0), chunk(a, xf, t, 0, r0, n))
-        recv(("xf", r, 1), chunk(a, xf, t, 1, r0, n))
+        send(("s", r), p, p, d_sib)
+        recv(("xf", r), chunk(a, xf, t, 0, r0, n), chunk(a, xf, t, 1, r0, n))
         p = part(a, xf, core, t, r0, n)
-        send(("s", r, 3), p, p, d_sib)
+        send(("s", r), p, p, d_sib)
 
     def sfin(r):
         a, rel, r0, n = ROUNDS[r]
-        for j, xp in enumerate(xorder):
-            recv(("s", r, j), part(a, xp, oc, t_of[rel], r0, n))
+        recv(("s", r), *[part(a, xp, oc, t_of[rel], r0, n) for xp in xorder])
 
     def forward(a, rel, r0, n):
         t = t_of[rel]
@@ -332,7 +351,7 @@
     sfin(0)
     hz_inner(3)
     forward(0, 0, 0, R)
-    send("pgu", pgu.at[0], pgur, d_zhi)
+    send("ex", pgu.at[0], pgur, d_zhi)
     yfwd(1)
     xfwd(1)
     xfwd(3)
@@ -341,7 +360,7 @@
     hsfin(0)
     yfin(1)
     forward(1, 0, 0, R)
-    send("ph", ph.at[0], phr, d_zhi)
+    send("ex", ph.at[0], phr, d_zhi)
     xfin(1)
     for j in range(4):
         hz_outer(j)
@@ -353,8 +372,7 @@
     sfin(3)
     forward(1, 1, *REST)
 
-    recv("pgu", pgur)
-    recv("ph", phr)
+    recv("ex", pgur, phr)
     gate = pgu[1, :, :F] + pgur[:, :F]
     up = pgu[1, :, F:] + pgur[:, F:]
     hg = ph[1] + phr[...]
@@ -364,8 +382,8 @@
     agu[trow(1 - z_hi), :F] = (hg * up * slope).astype(BF)
     agu[trow(1 - z_hi), F:] = (hg * activated).astype(BF)
     ah[trow(1 - z_hi), :] = (activated * up).astype(BF)
-    send("agu", agu.at[trow(1 - z_hi), :], agu.at[trow(1 - z_hi), :], d_zhi)
-    send("ah", ah.at[trow(1 - z_hi), :], ah.at[trow(1 - z_hi), :], d_zhi)
+    send("act", agu.at[trow(1 - z_hi), :], agu.at[trow(1 - z_hi), :], d_zhi)
+    send("act", ah.at[trow(1 - z_hi), :], ah.at[trow(1 - z_hi), :], d_zhi)
 
     order = (xf, xr, xl, x)
     RA = ((ZF, R - ZF), (0, ZF))
@@ -405,7 +423,7 @@
 
     def ignear(p, rel, k):
         for h, (xp, d) in enumerate(((xr, d_xr), (xl, d_xl))):
-            send(("in", k, h, 1 - h), igp.at[rel, 2 * xp + core, hrows(p, 1 - h), :],
+            send(("in", k), igp.at[rel, 2 * xp + core, hrows(p, 1 - h), :],
                  nearr.at[rel, h, hrows(p, 1 - h), :], d)
 
     def igsecond(p, rel, k):
@@ -413,12 +431,10 @@
             n = pl.ds(0, RA[p][1] // 2)
             recv(("if", k, h), farr.at[k, h, n, :])
             igp[rel, 2 * xp + core, hrows(p, h), :] += farr[k, h, n, :].astype(F32)
-            send(("in", k, h, h), igp.at[rel, 2 * xp + core, hrows(p, h), :], nearr.at[rel, h, hrows(p, h), :], d)
+            send(("in", k), igp.at[rel, 2 * xp + core, hrows(p, h), :], nearr.at[rel, h, hrows(p, h), :], d)
 
     def iglast(p, rel, k):
-        for h in range(2):
-            for g in range(2):
-                recv(("in", k, h, g), nearr.at[rel, h, hrows(p, g), :])
+        recv(("in", k), *[nearr.at[rel, h, hrows(p, g), :] for h in range(2) for g in range(2)])
         igp[rel, 2 * x + core, arows(p), :] += nearr[rel, 0, arows(p), :] + nearr[rel, 1, arows(p), :]
 
     def igfirst(rel, when):
@@ -446,12 +462,12 @@
     def zsend(rel):
         for h in range(2):
             send(("zi", rel, h), igp.at[rel, 2 * x + core, hrows(0, h), :], zr.at[hrows(0, h), :], d_zlo,
-                 rs=sid(("zir", h)), wait_later=False)
+                 rs=slot(recvs, ("zir", h)), wait_later=False)
 
     def wfirst(e, s, h):
         wunit(e)
-        send(("gn", s, h), gb.at[e], gnr.at[s, h], sides[s][1])
-        send(("hn", s, h), hb.at[e], hnr.at[s, h], sides[s][1])
+        send("gn", gb.at[e], gnr.at[s, h], sides[s][1])
+        send("gn", hb.at[e], hnr.at[s, h], sides[s][1])
 
     def zfadd(j):
         xp = order[j]
@@ -460,22 +476,20 @@
 
     def wsecond(h):
         yp, d = sides[h]
-        recv(("gf", h), gfr.at[h])
+        recv(("gf", h), gfr.at[h], hfr.at[h])
         gb[2 * yp + h] = (ws[2 * yp + h] + gfr[h].astype(F32)).astype(BF)
-        send(("gn", h, h), gb.at[2 * yp + h], gnr.at[h, h], d)
-        recv(("hf2", h), hfr.at[h])
+        send("gn", gb.at[2 * yp + h], gnr.at[h, h], d)
         hb[2 * yp + h] = (hs[2 * yp + h] + hfr[h].astype(F32)).astype(BF)
-        send(("hn", h, h), hb.at[2 * yp + h], hnr.at[h, h], d)
+        send("gn", hb.at[2 * yp + h], hnr.at[h, h], d)
 
     keep = inner
     igstart(1)
     igfirst(1, is_outer)
-    recv("agu", agu.at[trow(z_hi), :])
-    recv("ah", ah.at[trow(z_hi), :])
+    recv("act", agu.at[trow(z_hi), :], ah.at[trow(z_hi), :])
     for h, (yp, d) in enumerate(sides):
         wunit(2 * yf + h)
         send(("gf", h), gb.at[2 * yf + h], gfr.at[h], d)
-        send(("hf2", h), hb.at[2 * yf + h], hfr.at[h], d)
+        send(("gf", h), hb.at[2 * yf + h], hfr.at[h], d)
     igsecond(0, 1, 1)
     igstart(0)
     igfirst(0, is_inner)
@@ -523,10 +537,8 @@
     def _():
         ig_o[arows(1), :] = igp[0, 2 * x + core, arows(1), :].astype(BF)
 
+    recv("gn", *[b.at[s, h] for b in (gnr, hnr) for s in range(2) for h in range(2)])
     for h in range(2):
-        for s in range(2):
-            recv(("gn", s, h), gnr.at[s, h])
-            recv(("hn", s, h), hnr.at[s, h])
         g = (ws[2 * y + h] + gnr[0, h].astype(F32) + gnr[1, h].astype(F32)) * factor
         gg_o[pl.ds(h * C, C), :] = g[:, :F]
         ug_o[pl.ds(h * C, C), :] = g[:, F:]
@@ -537,12 +549,6 @@
         for h in range(2):
             recv(("zir", h), zr.at[hrows(0, h), :])
             ig_o[hrows(0, h), :] = (igp[0, 2 * x + core, hrows(0, h), :] + zr[hrows(0, h), :]).astype(BF)
-
-    def wait_send(name, src):
-        i = sid(name)
-        pltpu.make_async_remote_copy(
-            src_ref=src, dst_ref=src, send_sem=ssem.at[i], recv_sem=rsem.at[i],
-            device_id=d_sib, device_id_type=MESH).wait_send()
 
     @pl.when(is_inner)
     def _():
@@ -572,9 +578,9 @@
         wait_send(("zf", j), zfr.at[j])
         for rel in range(2):
             wait_send(("hs", rel, j), hpart(rel, j))
-    for c in pending:
-        c.wait_send()
-    assert len(ids) <= NSEM
+    for k, sizes in enumerate(groups):
+        wait_bytes(ssem.at[slot(sends, ("group", k))], sum(sizes))
+    assert len(sends) <= NSEND and len(recvs) <= NRECV, (len(sends), len(recvs))
 
 
 def deliver(*refs):
@@ -602,7 +608,7 @@
         V((R, C), F32), V((3, H, C), BF), V((3, H, C), BF),
         V((8, C, 2 * F), F32), V((8, F, C), F32), V((8, C, 2 * F), BF), V((8, F, C), BF),
         V((2, C, 2 * F), BF), V((2, F, C), BF), V((2, 2, C, 2 * F), BF), V((2, 2, F, C), BF),
-        pltpu.SemaphoreType.DMA((8,)), pltpu.SemaphoreType.DMA((NSEM,)), pltpu.SemaphoreType.DMA((NSEM,)),
+        pltpu.SemaphoreType.DMA((8,)), pltpu.SemaphoreType.DMA((NSEND,)), pltpu.SemaphoreType.DMA((NRECV,)),
     ]
     held = pl.pallas_call(
         functools.partial(kernel, factor),

time: 84.8 us -> 82 us (0.967)
  Pallas kernels: 83.9 us -> 81 us
    pallas_call x1, Pallas kernels: 82.6 us -> 79.8 us  [shards(): pl.pallas_call(functools.partial(kernel, factor), out_shape=(V((R, C), BF...]
where the time goes in v7:
time: 82 us; the launch traced here: 81.7 us
  Pallas kernels  81 us (99%)
    pallas_call x1, Pallas kernels, shards(): pl.pallas_call(functools.partial(kernel, factor), out_shape=(V((R, C), BF...  79.8 us

profile of v7, /device:TPU:1, one launch (start us, length us, event | category | flops | bytes accessed | tf_op | source)
XLA Modules:
  0.0 81.7 jit_solution(13434087017540021911)
XLA Ops:
  0.6 79.8 %ffn_backward.1 = (bf16[256,512]{1,0:T(8,128)(2,1)S(1)}, f32[1024,128]{1,0:T(8,128)S(1)}, f32[1024,128]{1,0:T(8,128)S(1)}, f32[128,1024]{1,0:T(8,128)S(1)}) custom-call(bf16[256,512]{1,0:T(8,128)(2,1)} %tok.1, bf16[256,512]{1,0:T(8,128)(2,1)} %og.1, bf16[1024,128]{1,0:T(8,128)(2,1)} %wg.1, bf16[1024,128]{1,0:T(8,128)(2,1)} %wu.1, bf16[128,1024]{1,0:T(8,128)(2,1)} %wd.1), custom_call_target="tpu_custom_call" | custom-call | tf_op jit(solution)/shard_map/ffn_backward/pallas_call | solution.py:613
  80.4 1.3 %deliver.1 = (bf16[256,512]{1,0:T(8,128)(2,1)}, f32[1024,128]{1,0:T(8,128)}, f32[1024,128]{1,0:T(8,128)}, f32[128,1024]{1,0:T(8,128)}) custom-call(bf16[256,512]{1,0:T(8,128)(2,1)S(1)} %get-tuple-element.8.refs_0_, f32[1024,128]{1,0:T(8,128)S(1)} %get-tuple-element.9.refs_1_, f32[1024,128]{1,0:T(8,128)S(1)} %get-tuple-element.10.refs_2_, ...), custom_call_target="tpu_custom_call" | custom-call | tf_op jit(solution)/shard_map/deliver/pallas_call | solution.py:628

commit v8 on v7

--- a/solution.py
+++ b/solution.py
@@ -16,6 +16,7 @@
 F32 = jnp.float32
 NSEND, NRECV = 48, 96
 GROUP = 6
+ROUNDED = (0, 1, 2)
 ZF = 64
 HOME = 160
 ROUNDS = ((0, 0, 0, 256), (0, 1, 0, 256), (1, 0, HOME, 256 - HOME), (1, 1, HOME, 256 - HOME))
@@ -26,7 +27,7 @@
 
 
 def kernel(factor, tok, og, wg, wu, wd, ig_o, gg_o, ug_o, dg_o,
-           own, xb, wgu, wdn, pgu, ph, pgur, phr, agu, ah, igp, sibr, farr, nearr, fs, zfr, zr, igs, igr,
+           own, xb, wgu, wdn, pgu, ph, pgur, phr, agu, ah, igp, sibr, farr, nearr, fs, ns, nowr, zfr, zr, igs, igr,
            ws, hs, gb, hb, gfr, hfr, gnr, hnr, lsem, ssem, rsem):
     R, C = tok.shape
     F = wg.shape[1]
@@ -324,6 +325,9 @@
         (pgu, ph)[a][rel, pl.ds(r0, n)] = functools.reduce(jnp.add, terms)
 
     REST = (HOME, R - HOME)
+
+    def gate_up():
+        return pgu[1, :, :F] + pgur[:, :F], pgu[1, :, F:] + pgur[:, F:]
 
     hsend()
     ysend(0)
@@ -351,7 +355,7 @@
     sfin(0)
     hz_inner(3)
     forward(0, 0, 0, R)
-    send("ex", pgu.at[0], pgur, d_zhi)
+    send("exg", pgu.at[0], pgur, d_zhi)
     yfwd(1)
     xfwd(1)
     xfwd(3)
@@ -360,30 +364,32 @@
     hsfin(0)
     yfin(1)
     forward(1, 0, 0, R)
-    send("ex", ph.at[0], phr, d_zhi)
+    send("exh", ph.at[0], phr, d_zhi)
     xfin(1)
     for j in range(4):
         hz_outer(j)
     xfin(3)
     sfin(1)
     forward(0, 1, 0, R)
+    recv("exg", pgur)
+    mine, away = trow(1 - z_hi), trow(z_hi)
+    gate, up = gate_up()
+    ah[mine, :] = (gate * jax.nn.sigmoid(gate) * up).astype(BF)
+    send("acth", ah.at[mine, :], ah.at[mine, :], d_zhi)
     hsfin(1)
     forward(1, 1, 0, HOME)
     sfin(3)
     forward(1, 1, *REST)
 
-    recv("ex", pgur, phr)
-    gate = pgu[1, :, :F] + pgur[:, :F]
-    up = pgu[1, :, F:] + pgur[:, F:]
+    recv("exh", phr)
+    gate, up = gate_up()
     hg = ph[1] + phr[...]
     squashed = jax.nn.sigmoid(gate)
     activated = gate * squashed
     slope = squashed * (1.0 + gate * (1.0 - squashed))
-    agu[trow(1 - z_hi), :F] = (hg * up * slope).astype(BF)
-    agu[trow(1 - z_hi), F:] = (hg * activated).astype(BF)
-    ah[trow(1 - z_hi), :] = (activated * up).astype(BF)
-    send("act", agu.at[trow(1 - z_hi), :], agu.at[trow(1 - z_hi), :], d_zhi)
-    send("act", ah.at[trow(1 - z_hi), :], ah.at[trow(1 - z_hi), :], d_zhi)
+    agu[mine, :F] = (hg * up * slope).astype(BF)
+    agu[mine, F:] = (hg * activated).astype(BF)
+    send("actg", agu.at[mine, :], agu.at[mine, :], d_zhi)
 
     order = (xf, xr, xl, x)
     RA = ((ZF, R - ZF), (0, ZF))
@@ -422,9 +428,14 @@
             send(("if", k, h), fs.at[k, h, n, :], farr.at[k, h, n, :], d)
 
     def ignear(p, rel, k):
+        n = pl.ds(0, RA[p][1] // 2)
         for h, (xp, d) in enumerate(((xr, d_xr), (xl, d_xl))):
-            send(("in", k), igp.at[rel, 2 * xp + core, hrows(p, 1 - h), :],
-                 nearr.at[rel, h, hrows(p, 1 - h), :], d)
+            rows_h = hrows(p, 1 - h)
+            if k in ROUNDED:
+                ns[k, h, n, :] = igp[rel, 2 * xp + core, rows_h, :].astype(BF)
+                send(("in", k), ns.at[k, h, n, :], nowr.at[k, h, n, :], d)
+            else:
+                send(("in", k), igp.at[rel, 2 * xp + core, rows_h, :], nearr.at[rel, h, rows_h, :], d)
 
     def igsecond(p, rel, k):
         for h, (xp, d) in enumerate(((xr, d_xr), (xl, d_xl))):
@@ -434,8 +445,12 @@
             send(("in", k), igp.at[rel, 2 * xp + core, hrows(p, h), :], nearr.at[rel, h, hrows(p, h), :], d)
 
     def iglast(p, rel, k):
-        recv(("in", k), *[nearr.at[rel, h, hrows(p, g), :] for h in range(2) for g in range(2)])
-        igp[rel, 2 * x + core, arows(p), :] += nearr[rel, 0, arows(p), :] + nearr[rel, 1, arows(p), :]
+        n = pl.ds(0, RA[p][1] // 2)
+        first = [nowr.at[k, h, n, :] if k in ROUNDED else nearr.at[rel, h, hrows(p, 1 - h), :] for h in range(2)]
+        second = [nearr.at[rel, h, hrows(p, h), :] for h in range(2)]
+        recv(("in", k), *first, *second)
+        for h in range(2):
+            igp[rel, 2 * x + core, hrows(p, h), :] += second[h][...] + first[1 - h][...].astype(F32)
 
     def igfirst(rel, when):
         addsib(rel, 0)
@@ -450,10 +465,12 @@
             for j in range(4):
                 zfirst(rel, j)
 
-    def wunit(e):
+    def gunit(e):
         g = dot(xb[0, e, : 2 * R], agu[...], 0, 0)
         ws[e] = g
         gb[e] = g.astype(BF)
+
+    def hunit(e):
         d = dot(ah[...], xb[1, e, : 2 * R], 0, 0)
         hs[e] = d
         hb[e] = d.astype(BF)
@@ -463,40 +480,50 @@
         for h in range(2):
             send(("zi", rel, h), igp.at[rel, 2 * x + core, hrows(0, h), :], zr.at[hrows(0, h), :], d_zlo,
                  rs=slot(recvs, ("zir", h)), wait_later=False)
-
-    def wfirst(e, s, h):
-        wunit(e)
-        send("gn", gb.at[e], gnr.at[s, h], sides[s][1])
-        send("gn", hb.at[e], hnr.at[s, h], sides[s][1])
 
     def zfadd(j):
         xp = order[j]
         recv(("zf", j), zfr.at[xp])
         igp[keep, 2 * xp + core, arows(1), :] += zfr[xp]
 
-    def wsecond(h):
+    def hsecond(h):
         yp, d = sides[h]
-        recv(("gf", h), gfr.at[h], hfr.at[h])
+        recv(("hf", h), hfr.at[h])
+        hb[2 * yp + h] = (hs[2 * yp + h] + hfr[h].astype(F32)).astype(BF)
+        send("gn", hb.at[2 * yp + h], hnr.at[h, h], d)
+
+    def gsecond(h):
+        yp, d = sides[h]
+        recv(("gf", h), gfr.at[h])
         gb[2 * yp + h] = (ws[2 * yp + h] + gfr[h].astype(F32)).astype(BF)
         send("gn", gb.at[2 * yp + h], gnr.at[h, h], d)
-        hb[2 * yp + h] = (hs[2 * yp + h] + hfr[h].astype(F32)).astype(BF)
-        send("gn", hb.at[2 * yp + h], hnr.at[h, h], d)
 
     keep = inner
     igstart(1)
+    recv("acth", ah.at[away, :])
+    for h, (yp, d) in enumerate(sides):
+        hunit(2 * yf + h)
+        send(("hf", h), hb.at[2 * yf + h], hfr.at[h], d)
     igfirst(1, is_outer)
-    recv("act", agu.at[trow(z_hi), :], ah.at[trow(z_hi), :])
     for h, (yp, d) in enumerate(sides):
-        wunit(2 * yf + h)
+        hunit(2 * yp + 1 - h)
+        send("gn", hb.at[2 * yp + 1 - h], hnr.at[h, 1 - h], d)
+    recv("actg", agu.at[away, :])
+    for h, (yp, d) in enumerate(sides):
+        gunit(2 * yf + h)
         send(("gf", h), gb.at[2 * yf + h], gfr.at[h], d)
-        send(("gf", h), hb.at[2 * yf + h], hfr.at[h], d)
     igsecond(0, 1, 1)
     igstart(0)
+    for h, (yp, d) in enumerate(sides):
+        hunit(2 * yp + h)
     igfirst(0, is_inner)
     for h, (yp, d) in enumerate(sides):
-        wfirst(2 * yp + 1 - h, h, 1 - h)
+        gunit(2 * yp + 1 - h)
+        send("gn", gb.at[2 * yp + 1 - h], gnr.at[h, 1 - h], d)
+    for h in range(2):
+        hsecond(h)
     for h, (yp, d) in enumerate(sides):
-        wunit(2 * yp + h)
+        gunit(2 * yp + h)
     iglast(0, 1, 1)
 
     @pl.when(is_outer)
@@ -505,14 +532,15 @@
 
     zfadd(0)
     igfar(1, keep, 2)
-    wsecond(0)
-    wsecond(1)
+    gsecond(0)
+    gsecond(1)
     igsecond(0, 0, 0)
     zfadd(1)
     zfadd(2)
     ignear(1, keep, 2)
     for h in range(2):
-        wunit(2 * y + h)
+        gunit(2 * y + h)
+        hunit(2 * y + h)
     igsecond(1, keep, 2)
     iglast(0, 0, 0)
 
@@ -604,7 +632,7 @@
         V((2, R, C), BF), V((2, 8, 2 * R + HOME, C), BF), V((4, 2 * C, 2 * F), BF), V((4, F, 2 * C), BF),
         V((2, R, 2 * F), F32), V((2, R, F), F32), V((R, 2 * F), F32), V((R, F), F32),
         V((2 * R, 2 * F), BF), V((2 * R, F), BF),
-        V((2, 8, R, C), F32), V((2, 4, R, C), F32), V((3, 2, H, C), BF), V((2, 2, R, C), F32), V((3, 2, H, C), BF), V((4, ZF, C), F32),
+        V((2, 8, R, C), F32), V((2, 4, R, C), F32), V((3, 2, H, C), BF), V((2, 2, R, C), F32), V((3, 2, H, C), BF), V((3, 2, H, C), BF), V((3, 2, H, C), BF), V((4, ZF, C), F32),
         V((R, C), F32), V((3, H, C), BF), V((3, H, C), BF),
         V((8, C, 2 * F), F32), V((8, F, C), F32), V((8, C, 2 * F), BF), V((8, F, C), BF),
         V((2, C, 2 * F), BF), V((2, F, C), BF), V((2, 2, C, 2 * F), BF), V((2, 2, F, C), BF),

time: 82 us -> 79 us (0.963)
  Pallas kernels: 81 us -> 78.1 us
    pallas_call x1, Pallas kernels: 79.8 us -> 76.8 us  [shards(): pl.pallas_call(functools.partial(kernel, factor), out_shape=(V((R, C), BF...]
where the time goes in v8:
time: 79 us; the launch traced here: 78.7 us
  Pallas kernels  78.1 us (99%)
    pallas_call x1, Pallas kernels, shards(): pl.pallas_call(functools.partial(kernel, factor), out_shape=(V((R, C), BF...  76.8 us

profile of v8, /device:TPU:1, one launch (start us, length us, event | category | flops | bytes accessed | tf_op | source)
XLA Modules:
  0.0 78.7 jit_solution(9303886375030325108)
XLA Ops:
  0.6 76.8 %ffn_backward.1 = (bf16[256,512]{1,0:T(8,128)(2,1)S(1)}, f32[1024,128]{1,0:T(8,128)S(1)}, f32[1024,128]{1,0:T(8,128)S(1)}, f32[128,1024]{1,0:T(8,128)S(1)}) custom-call(bf16[256,512]{1,0:T(8,128)(2,1)} %tok.1, bf16[256,512]{1,0:T(8,128)(2,1)} %og.1, bf16[1024,128]{1,0:T(8,128)(2,1)} %wg.1, bf16[1024,128]{1,0:T(8,128)(2,1)} %wu.1, bf16[128,1024]{1,0:T(8,128)(2,1)} %wd.1), custom_call_target="tpu_custom_call" | custom-call | tf_op jit(solution)/shard_map/ffn_backward/pallas_call | solution.py:641
  77.4 1.3 %deliver.1 = (bf16[256,512]{1,0:T(8,128)(2,1)}, f32[1024,128]{1,0:T(8,128)}, f32[1024,128]{1,0:T(8,128)}, f32[128,1024]{1,0:T(8,128)}) custom-call(bf16[256,512]{1,0:T(8,128)(2,1)S(1)} %get-tuple-element.8.refs_0_, f32[1024,128]{1,0:T(8,128)S(1)} %get-tuple-element.9.refs_1_, f32[1024,128]{1,0:T(8,128)S(1)} %get-tuple-element.10.refs_2_, ...), custom_call_target="tpu_custom_call" | custom-call | tf_op jit(solution)/shard_map/deliver/pallas_call | solution.py:656

commit v9 on v8

--- a/solution.py
+++ b/solution.py
@@ -14,7 +14,7 @@
 MESH = pl.DeviceIdType.MESH
 BF = jnp.bfloat16
 F32 = jnp.float32
-NSEND, NRECV = 48, 96
+NSEND, NRECV = 23, 88
 GROUP = 6
 ROUNDED = (0, 1, 2)
 ZF = 64
@@ -98,9 +98,6 @@
         else:
             wait_bytes(rsem.at[slot(recvs, name)], sum(size(d) for d in dsts))
 
-    def wait_send(name, src):
-        remote(src, src, d_sib, slot(sends, name), 0).wait_send()
-
     def trow(t):
         return pl.ds(pl.multiple_of(t * R, R), R)
 
@@ -220,13 +217,13 @@
         return part(1, xorder[j], core, t_of[rel], 0, HOME)
 
     def hsib(rel, j):
-        send(("hs", rel, j), hpart(rel, j), hpart(rel, j), d_sib, rs=slot(recvs, ("hs", rel)), wait_later=False)
+        send("hs", hpart(rel, j), hpart(rel, j), d_sib, rs=slot(recvs, ("hs", rel)), wait_later=False)
 
     def hz_inner(j):
         @pl.when(is_inner)
         def _():
             recv(("zh", 4 + j), hpart(1, j))
-            send(("hzr", j), hpart(1, j), hpart(1, j), d_zlo, rs=12 + j, wait_later=False)
+            send("zrel", hpart(1, j), hpart(1, j), d_zlo, rs=12 + j, wait_later=False)
             hsib(1, j)
             recv(("zh", j), hpart(0, j))
             hsib(0, j)
@@ -256,7 +253,7 @@
             def _():
                 c = chunk(a, x, t, h, r0, n)
                 recv(("z", 4 + k), c)
-                send(("zr", k), c, c, d_zlo, rs=4 + k, wait_later=False)
+                send("zrel", c, c, d_zlo, rs=4 + k, wait_later=False)
 
     def xsend_h(r, h):
         a, rel, r0, n = ROUNDS[r]
@@ -419,7 +416,8 @@
 
     def zfirst(rel, j):
         xp = order[j]
-        send(("zf", j), igp.at[rel, 2 * xp + core, arows(1), :], zfr.at[xp], d_zlo, wait_later=False)
+        send("zf", igp.at[rel, 2 * xp + core, arows(1), :], zfr.at[xp], d_zlo,
+             rs=slot(recvs, ("zf", j)), wait_later=False)
 
     def igfar(p, rel, k):
         for h, d in enumerate((d_xr, d_xl)):
@@ -478,7 +476,7 @@
     sides = ((yr, d_yr), (yl, d_yl))
     def zsend(rel):
         for h in range(2):
-            send(("zi", rel, h), igp.at[rel, 2 * x + core, hrows(0, h), :], zr.at[hrows(0, h), :], d_zlo,
+            send("zi", igp.at[rel, 2 * x + core, hrows(0, h), :], zr.at[hrows(0, h), :], d_zlo,
                  rs=slot(recvs, ("zir", h)), wait_later=False)
 
     def zfadd(j):
@@ -547,19 +545,21 @@
     @pl.when(is_inner)
     def _():
         zsend(0)
+
+    zfadd(3)
+    iglast(1, keep, 2)
+
+    @pl.when(is_inner)
+    def _():
+        igs[2, pl.ds(0, ZF), :] = igp[1, 2 * x + core, arows(1), :].astype(BF)
+        send("zo", igs.at[2, pl.ds(0, ZF), :], igr.at[2, pl.ds(0, ZF), :], d_zz,
+             rs=slot(recvs, ("zo", 2)), wait_later=False)
         n = pl.ds(0, (R - ZF) // 2)
         for h in range(2):
             recv(("zir", h), zr.at[hrows(0, h), :])
             igs[h, n, :] = (igp[1, 2 * x + core, hrows(0, h), :] + zr[hrows(0, h), :]).astype(BF)
-            send(("zo", h), igs.at[h, n, :], igr.at[h, n, :], d_zz, wait_later=False)
-
-    zfadd(3)
-    iglast(1, keep, 2)
-
-    @pl.when(is_inner)
-    def _():
-        igs[2, pl.ds(0, ZF), :] = igp[1, 2 * x + core, arows(1), :].astype(BF)
-        send(("zo", 2), igs.at[2, pl.ds(0, ZF), :], igr.at[2, pl.ds(0, ZF), :], d_zz, wait_later=False)
+            send("zo", igs.at[h, n, :], igr.at[h, n, :], d_zz,
+                 rs=slot(recvs, ("zo", h)), wait_later=False)
 
     @pl.when(is_outer)
     def _():
@@ -586,26 +586,13 @@
         for h in range(2):
             recv(("zo", h), igr.at[h, n, :])
             ig_o[hrows(0, h), :] = igr[h, n, :]
-        wait_send(("zo", 2), igs.at[2, zs, :])
-        for h in range(2):
-            wait_send(("zo", h), igs.at[h, n, :])
-            wait_send(("zi", 0, h), zr.at[hrows(0, h), :])
-        for r in (1, 3):
-            a, rel, r0, n = ROUNDS[r]
-            for h in range(2):
-                wait_send(("zr", 2 * a + h), chunk(a, x, t_of[1], h, r0, n))
-        for j in range(4):
-            wait_send(("hzr", j), hpart(1, j))
-
-    @pl.when(is_outer)
-    def _():
-        for h in range(2):
-            wait_send(("zi", 1, h), zr.at[hrows(0, h), :])
-
-    for j in range(4):
-        wait_send(("zf", j), zfr.at[j])
-        for rel in range(2):
-            wait_send(("hs", rel, j), hpart(rel, j))
+        wait_bytes(ssem.at[slot(sends, "zo")], R * C * 2)
+        relayed = (ROUNDS[1][3] + ROUNDS[3][3] + 4 * HOME) * C * 2
+        wait_bytes(ssem.at[slot(sends, "zrel")], relayed)
+
+    wait_bytes(ssem.at[slot(sends, "zi")], (R - ZF) * C * 4)
+    wait_bytes(ssem.at[slot(sends, "zf")], 4 * ZF * C * 4)
+    wait_bytes(ssem.at[slot(sends, "hs")], 8 * HOME * C * 2)
     for k, sizes in enumerate(groups):
         wait_bytes(ssem.at[slot(sends, ("group", k))], sum(sizes))
     assert len(sends) <= NSEND and len(recvs) <= NRECV, (len(sends), len(recvs))

time: 79 us -> 78.7 us (level)
  no operation moved by 1% of the time
where the time goes in v9:
time: 78.7 us; the launch traced here: 78.4 us
  Pallas kernels  77.7 us (99%)
    pallas_call x1, Pallas kernels, shards(): pl.pallas_call(functools.partial(kernel, factor), out_shape=(V((R, C), BF...  76.5 us

profile of v9, /device:TPU:1, one launch (start us, length us, event | category | flops | bytes accessed | tf_op | source)
XLA Modules:
  0.0 78.4 jit_solution(18163873178809825594)
XLA Ops:
  0.6 76.5 %ffn_backward.1 = (bf16[256,512]{1,0:T(8,128)(2,1)S(1)}, f32[1024,128]{1,0:T(8,128)S(1)}, f32[1024,128]{1,0:T(8,128)S(1)}, f32[128,1024]{1,0:T(8,128)S(1)}) custom-call(bf16[256,512]{1,0:T(8,128)(2,1)} %tok.1, bf16[256,512]{1,0:T(8,128)(2,1)} %og.1, bf16[1024,128]{1,0:T(8,128)(2,1)} %wg.1, bf16[1024,128]{1,0:T(8,128)(2,1)} %wu.1, bf16[128,1024]{1,0:T(8,128)(2,1)} %wd.1), custom_call_target="tpu_custom_call" | custom-call | tf_op jit(solution)/shard_map/ffn_backward/pallas_call | solution.py:628
  77.1 1.3 %deliver.1 = (bf16[256,512]{1,0:T(8,128)(2,1)}, f32[1024,128]{1,0:T(8,128)}, f32[1024,128]{1,0:T(8,128)}, f32[128,1024]{1,0:T(8,128)}) custom-call(bf16[256,512]{1,0:T(8,128)(2,1)S(1)} %get-tuple-element.8.refs_0_, f32[1024,128]{1,0:T(8,128)S(1)} %get-tuple-element.9.refs_1_, f32[1024,128]{1,0:T(8,128)S(1)} %get-tuple-element.10.refs_2_, ...), custom_call_target="tpu_custom_call" | custom-call | tf_op jit(solution)/shard_map/deliver/pallas_call | solution.py:643

commit v10 on v9

--- a/solution.py
+++ b/solution.py
@@ -16,7 +16,7 @@
 F32 = jnp.float32
 NSEND, NRECV = 23, 88
 GROUP = 6
-ROUNDED = (0, 1, 2)
+ROUNDED = (0, 1)
 ZF = 64
 HOME = 160
 ROUNDS = ((0, 0, 0, 256), (0, 1, 0, 256), (1, 0, HOME, 256 - HOME), (1, 1, HOME, 256 - HOME))
@@ -406,6 +406,8 @@
         for j, xp in enumerate(order):
             igblock(rel, xp, oc)
             send(("is", rel, j), igp.at[rel, 2 * xp + oc], sibr.at[rel, xp], d_sib)
+
+    def igown(rel):
         for xp in order:
             igblock(rel, xp, core)
 
@@ -498,6 +500,7 @@
 
     keep = inner
     igstart(1)
+    igown(1)
     recv("acth", ah.at[away, :])
     for h, (yp, d) in enumerate(sides):
         hunit(2 * yf + h)
@@ -510,8 +513,9 @@
     for h, (yp, d) in enumerate(sides):
         gunit(2 * yf + h)
         send(("gf", h), gb.at[2 * yf + h], gfr.at[h], d)
+    igstart(0)
     igsecond(0, 1, 1)
-    igstart(0)
+    igown(0)
     for h, (yp, d) in enumerate(sides):
         hunit(2 * yp + h)
     igfirst(0, is_inner)

time: 78.7 us -> 78.8 us (level)
  no operation moved by 1% of the time
where the time goes in v10:
time: 78.8 us; the launch traced here: 78.4 us
  Pallas kernels  77.7 us (99%)
    pallas_call x1, Pallas kernels, shards(): pl.pallas_call(functools.partial(kernel, factor), out_shape=(V((R, C), BF...  76.5 us

profile of v10, /device:TPU:1, one launch (start us, length us, event | category | flops | bytes accessed | tf_op | source)
XLA Modules:
  0.0 78.4 jit_solution(9392857856023546044)
XLA Ops:
  0.6 76.5 %ffn_backward.1 = (bf16[256,512]{1,0:T(8,128)(2,1)S(1)}, f32[1024,128]{1,0:T(8,128)S(1)}, f32[1024,128]{1,0:T(8,128)S(1)}, f32[128,1024]{1,0:T(8,128)S(1)}) custom-call(bf16[256,512]{1,0:T(8,128)(2,1)} %tok.1, bf16[256,512]{1,0:T(8,128)(2,1)} %og.1, bf16[1024,128]{1,0:T(8,128)(2,1)} %wg.1, bf16[1024,128]{1,0:T(8,128)(2,1)} %wu.1, bf16[128,1024]{1,0:T(8,128)(2,1)} %wd.1), custom_call_target="tpu_custom_call" | custom-call | tf_op jit(solution)/shard_map/ffn_backward/pallas_call | solution.py:632
  77.1 1.3 %deliver.1 = (bf16[256,512]{1,0:T(8,128)(2,1)}, f32[1024,128]{1,0:T(8,128)}, f32[1024,128]{1,0:T(8,128)}, f32[128,1024]{1,0:T(8,128)}) custom-call(bf16[256,512]{1,0:T(8,128)(2,1)S(1)} %get-tuple-element.8.refs_0_, f32[1024,128]{1,0:T(8,128)S(1)} %get-tuple-element.9.refs_1_, f32[1024,128]{1,0:T(8,128)S(1)} %get-tuple-element.10.refs_2_, ...), custom_call_target="tpu_custom_call" | custom-call | tf_op jit(solution)/shard_map/deliver/pallas_call | solution.py:647

commit v11 on v10

--- a/solution.py
+++ b/solution.py
@@ -16,7 +16,7 @@
 F32 = jnp.float32
 NSEND, NRECV = 23, 88
 GROUP = 6
-ROUNDED = (0, 1)
+ROUNDED = (0, 1, 2)
 ZF = 64
 HOME = 160
 ROUNDS = ((0, 0, 0, 256), (0, 1, 0, 256), (1, 0, HOME, 256 - HOME), (1, 1, HOME, 256 - HOME))
@@ -47,7 +47,7 @@
     d_zhi = (1 - z_hi, y, z_lo, x, core)
     d_zz = (1 - z_hi, y, 1 - z_lo, x, core)
     d_zs = (z_lo, y, 1 - z_lo, x, core)
-    partners = (d_xr, d_xl, d_yr, d_yl, d_sib, d_zlo, d_zhi, d_zz)
+    partners = (d_zhi, d_zlo, d_zz, d_xr, d_xl, d_yr, d_yl, d_sib)
 
     sends, recvs = {}, {}
 

time: 78.8 us -> 78.5 us (level)
  no operation moved by 1% of the time
where the time goes in v11:
time: 78.5 us; the launch traced here: 78.4 us
  Pallas kernels  77.8 us (99%)
    pallas_call x1, Pallas kernels, shards(): pl.pallas_call(functools.partial(kernel, factor), out_shape=(V((R, C), BF...  76.5 us

profile of v11, /device:TPU:1, one launch (start us, length us, event | category | flops | bytes accessed | tf_op | source)
XLA Modules:
  0.0 78.4 jit_solution(7259009437566953011)
XLA Ops:
  0.6 76.5 %ffn_backward.1 = (bf16[256,512]{1,0:T(8,128)(2,1)S(1)}, f32[1024,128]{1,0:T(8,128)S(1)}, f32[1024,128]{1,0:T(8,128)S(1)}, f32[128,1024]{1,0:T(8,128)S(1)}) custom-call(bf16[256,512]{1,0:T(8,128)(2,1)} %tok.1, bf16[256,512]{1,0:T(8,128)(2,1)} %og.1, bf16[1024,128]{1,0:T(8,128)(2,1)} %wg.1, bf16[1024,128]{1,0:T(8,128)(2,1)} %wu.1, bf16[128,1024]{1,0:T(8,128)(2,1)} %wd.1), custom_call_target="tpu_custom_call" | custom-call | tf_op jit(solution)/shard_map/ffn_backward/pallas_call | solution.py:632
  77.1 1.3 %deliver.1 = (bf16[256,512]{1,0:T(8,128)(2,1)}, f32[1024,128]{1,0:T(8,128)}, f32[1024,128]{1,0:T(8,128)}, f32[128,1024]{1,0:T(8,128)}) custom-call(bf16[256,512]{1,0:T(8,128)(2,1)S(1)} %get-tuple-element.8.refs_0_, f32[1024,128]{1,0:T(8,128)S(1)} %get-tuple-element.9.refs_1_, f32[1024,128]{1,0:T(8,128)S(1)} %get-tuple-element.10.refs_2_, ...), custom_call_target="tpu_custom_call" | custom-call | tf_op jit(solution)/shard_map/deliver/pallas_call | solution.py:647

commit v12 on v11

--- a/solution.py
+++ b/solution.py
@@ -16,7 +16,7 @@
 F32 = jnp.float32
 NSEND, NRECV = 23, 88
 GROUP = 6
-ROUNDED = (0, 1, 2)
+ROUNDED = (0, 1)
 ZF = 64
 HOME = 160
 ROUNDS = ((0, 0, 0, 256), (0, 1, 0, 256), (1, 0, HOME, 256 - HOME), (1, 1, HOME, 256 - HOME))

time: 78.5 us -> 78.9 us (level)
  no operation moved by 1% of the time
where the time goes in v12:
time: 78.9 us; the launch traced here: 78.4 us
  Pallas kernels  77.8 us (99%)
    pallas_call x1, Pallas kernels, shards(): pl.pallas_call(functools.partial(kernel, factor), out_shape=(V((R, C), BF...  76.5 us

profile of v12, /device:TPU:1, one launch (start us, length us, event | category | flops | bytes accessed | tf_op | source)
XLA Modules:
  0.0 78.4 jit_solution(15410036474437299083)
XLA Ops:
  0.6 76.5 %ffn_backward.1 = (bf16[256,512]{1,0:T(8,128)(2,1)S(1)}, f32[1024,128]{1,0:T(8,128)S(1)}, f32[1024,128]{1,0:T(8,128)S(1)}, f32[128,1024]{1,0:T(8,128)S(1)}) custom-call(bf16[256,512]{1,0:T(8,128)(2,1)} %tok.1, bf16[256,512]{1,0:T(8,128)(2,1)} %og.1, bf16[1024,128]{1,0:T(8,128)(2,1)} %wg.1, bf16[1024,128]{1,0:T(8,128)(2,1)} %wu.1, bf16[128,1024]{1,0:T(8,128)(2,1)} %wd.1), custom_call_target="tpu_custom_call" | custom-call | tf_op jit(solution)/shard_map/ffn_backward/pallas_call | solution.py:632
  77.1 1.3 %deliver.1 = (bf16[256,512]{1,0:T(8,128)(2,1)}, f32[1024,128]{1,0:T(8,128)}, f32[1024,128]{1,0:T(8,128)}, f32[128,1024]{1,0:T(8,128)}) custom-call(bf16[256,512]{1,0:T(8,128)(2,1)S(1)} %get-tuple-element.8.refs_0_, f32[1024,128]{1,0:T(8,128)S(1)} %get-tuple-element.9.refs_1_, f32[1024,128]{1,0:T(8,128)S(1)} %get-tuple-element.10.refs_2_, ...), custom_call_target="tpu_custom_call" | custom-call | tf_op jit(solution)/shard_map/deliver/pallas_call | solution.py:647

commit v13 on v11

--- a/solution.py
+++ b/solution.py
@@ -465,15 +465,19 @@
             for j in range(4):
                 zfirst(rel, j)
 
-    def gunit(e):
+    def gunit(e, send=True, sum=True):
         g = dot(xb[0, e, : 2 * R], agu[...], 0, 0)
-        ws[e] = g
-        gb[e] = g.astype(BF)
-
-    def hunit(e):
+        if sum:
+            ws[e] = g
+        if send:
+            gb[e] = g.astype(BF)
+
+    def hunit(e, send=True, sum=True):
         d = dot(ah[...], xb[1, e, : 2 * R], 0, 0)
-        hs[e] = d
-        hb[e] = d.astype(BF)
+        if sum:
+            hs[e] = d
+        if send:
+            hb[e] = d.astype(BF)
 
     sides = ((yr, d_yr), (yl, d_yl))
     def zsend(rel):
@@ -503,29 +507,29 @@
     igown(1)
     recv("acth", ah.at[away, :])
     for h, (yp, d) in enumerate(sides):
-        hunit(2 * yf + h)
+        hunit(2 * yf + h, sum=False)
         send(("hf", h), hb.at[2 * yf + h], hfr.at[h], d)
     igfirst(1, is_outer)
     for h, (yp, d) in enumerate(sides):
-        hunit(2 * yp + 1 - h)
+        hunit(2 * yp + 1 - h, sum=False)
         send("gn", hb.at[2 * yp + 1 - h], hnr.at[h, 1 - h], d)
     recv("actg", agu.at[away, :])
     for h, (yp, d) in enumerate(sides):
-        gunit(2 * yf + h)
+        gunit(2 * yf + h, sum=False)
         send(("gf", h), gb.at[2 * yf + h], gfr.at[h], d)
     igstart(0)
     igsecond(0, 1, 1)
     igown(0)
     for h, (yp, d) in enumerate(sides):
-        hunit(2 * yp + h)
+        hunit(2 * yp + h, send=False)
     igfirst(0, is_inner)
     for h, (yp, d) in enumerate(sides):
-        gunit(2 * yp + 1 - h)
+        gunit(2 * yp + 1 - h, sum=False)
         send("gn", gb.at[2 * yp + 1 - h], gnr.at[h, 1 - h], d)
     for h in range(2):
         hsecond(h)
     for h, (yp, d) in enumerate(sides):
-        gunit(2 * yp + h)
+        gunit(2 * yp + h, send=False)
     iglast(0, 1, 1)
 
     @pl.when(is_outer)
@@ -541,8 +545,8 @@
     zfadd(2)
     ignear(1, keep, 2)
     for h in range(2):
-        gunit(2 * y + h)
-        hunit(2 * y + h)
+        gunit(2 * y + h, send=False)
+        hunit(2 * y + h, send=False)
     igsecond(1, keep, 2)
     iglast(0, 0, 0)
 

time: 78.5 us -> 78.5 us (level)
  no operation moved by 1% of the time
where the time goes in v13:
time: 78.5 us; the launch traced here: 78.4 us
  Pallas kernels  77.8 us (99%)
    pallas_call x1, Pallas kernels, shards(): pl.pallas_call(functools.partial(kernel, factor), out_shape=(V((R, C), BF...  76.5 us

profile of v13, /device:TPU:1, one launch (start us, length us, event | category | flops | bytes accessed | tf_op | source)
XLA Modules:
  0.0 78.4 jit_solution(11973941874982425789)
XLA Ops:
  0.6 76.5 %ffn_backward.1 = (bf16[256,512]{1,0:T(8,128)(2,1)S(1)}, f32[1024,128]{1,0:T(8,128)S(1)}, f32[1024,128]{1,0:T(8,128)S(1)}, f32[128,1024]{1,0:T(8,128)S(1)}) custom-call(bf16[256,512]{1,0:T(8,128)(2,1)} %tok.1, bf16[256,512]{1,0:T(8,128)(2,1)} %og.1, bf16[1024,128]{1,0:T(8,128)(2,1)} %wg.1, bf16[1024,128]{1,0:T(8,128)(2,1)} %wu.1, bf16[128,1024]{1,0:T(8,128)(2,1)} %wd.1), custom_call_target="tpu_custom_call" | custom-call | tf_op jit(solution)/shard_map/ffn_backward/pallas_call | solution.py:636
  77.1 1.3 %deliver.1 = (bf16[256,512]{1,0:T(8,128)(2,1)}, f32[1024,128]{1,0:T(8,128)}, f32[1024,128]{1,0:T(8,128)}, f32[128,1024]{1,0:T(8,128)}) custom-call(bf16[256,512]{1,0:T(8,128)(2,1)S(1)} %get-tuple-element.8.refs_0_, f32[1024,128]{1,0:T(8,128)S(1)} %get-tuple-element.9.refs_1_, f32[1024,128]{1,0:T(8,128)S(1)} %get-tuple-element.10.refs_2_, ...), custom_call_target="tpu_custom_call" | custom-call | tf_op jit(solution)/shard_map/deliver/pallas_call | solution.py:651
